TPU v7x, 128 devices: a whole 4x4x4 slice. The times are simulated.
128 devices in a mesh: gx: 64 (over z, y, x), gy: 2 (over core).
Axes of the slice: x: 4, y: 4, z: 4, core: 2. Of those that a mesh axis runs over, the one named last changes fastest.
Arguments:
- history: bfloat16 [512, 2048, 256], P(('gx', 'gy')), may hold values from -100 to 100
- lengths: int32 [512], P(('gx', 'gy')), may hold values from 16 to 2048
- candidates: int32 [512, 64], P(('gx', 'gy')), may hold values from 0 to 524287, as said below
- item_table: bfloat16 [524288, 512], P(('gx', 'gy')), may hold values from -6 to 6
- value_weight: bfloat16 [256, 256], replicated, may hold values from -0.375 to 0.375
- click_hidden: bfloat16 [768, 256], replicated, may hold values from -0.21875 to 0.21875
- convert_hidden: bfloat16 [768, 256], replicated, may hold values from -0.21875 to 0.21875
- click_output: bfloat16 [256], replicated, may hold values from -0.75 to 0.75
- convert_output: bfloat16 [256], replicated, may hold values from -0.75 to 0.75
Outputs:
- click_rate: float32 [512, 64], P(('gx', 'gy'))
- click_conversion: float32 [512, 64], P(('gx', 'gy'))
Inputs may be any that keep to these rules, and one draw needn't show every extreme that they name: Device k holds the table rows k * 4096 to (k + 1) * 4096 - 1. Of the 256 candidates of one device, at most 4 are items of one device's rows, and exactly 4 are items of some device's rows.
All inputs are finite; a program needn't handle non-finite values.
Results may differ from a plain program's by a relative error of at most 0.0028.
Values may be sent and summed in bfloat16 or wider, within the bound.
No kernel may reach another device: no remote copies, remote signals or barrier semaphores. Data moves between devices by JAX's collectives and lax.ppermute only.
A program may use at most 64 MiB of HBM per device.

v0:
```python
import functools
import math

import jax
import jax.numpy as jnp
from jax import lax
from jax.experimental import pallas as pl
from jax.experimental.pallas import tpu as pltpu
from jax.sharding import PartitionSpec as P

HEADS = 4
SLOTS = 4
LANES = 128
CHUNK = 512
AXES = ("gx", "gy")
NEG = -1e30

F32 = jnp.float32
BF16 = jnp.bfloat16


def iota(shape, dim):
    return lax.broadcasted_iota(jnp.int32, shape, dim)


def ones_where(cond):
    return jnp.where(cond, 1.0, 0.0).astype(BF16)


def mm(a, b):
    return lax.dot_general(a, b, (((1,), (0,)), ((), ())), preferred_element_type=F32)


def mm_nt(a, b):
    return lax.dot_general(a, b, (((1,), (1,)), ((), ())), preferred_element_type=F32)


def request_kernel(cand_ref, req_ref, slot_ref, *, owners, row_bits):
    users, cands = cand_ref.shape
    total = users * cands
    ids = jnp.concatenate([cand_ref[u : u + 1, :] for u in range(users)], axis=1)
    owner = lax.shift_right_logical(ids, row_bits)
    row = jnp.bitwise_and(ids, (1 << row_bits) - 1)
    high = lax.shift_right_logical(row, 8).astype(F32)
    low = jnp.bitwise_and(row, 255).astype(F32)
    match = iota((owners, total), 0) == owner
    before = ones_where(iota((total, total), 0) < iota((total, total), 1))
    rank = mm(ones_where(match), before)
    place = jnp.sum(jnp.where(match, rank, 0.0), axis=0, keepdims=True) + (owner * SLOTS).astype(F32)
    slot_ref[...] = jnp.broadcast_to(place, slot_ref.shape)
    lane = iota((LANES, total), 0)
    picks, values = [], []
    for s in range(SLOTS):
        picks.append(ones_where(match & (rank == float(s))))
        values.append(
            jnp.where(lane == 2 * s, high, jnp.where(lane == 2 * s + 1, low, 0.0)).astype(BF16)
        )
    req_ref[...] = mm_nt(jnp.concatenate(picks, axis=1), jnp.concatenate(values, axis=1))


def answer_kernel(req_ref, staged_ref, table_ref, out_ref, hot_ref, high_ref, acc_ref, rest_ref, sem_ref):
    sources = req_ref.shape[0]
    rows = sources * SLOTS
    staged, width = staged_ref.shape
    rest = pltpu.make_async_copy(table_ref.at[pl.ds(staged, rest_ref.shape[0])], rest_ref, sem_ref)
    rest.start()
    spread = ones_where(lax.shift_right_logical(iota((rows, sources), 0), 2) == iota((rows, sources), 1))
    asked = mm(spread, req_ref[...].astype(BF16))
    own = lax.shift_right_logical(iota((rows, LANES), 1), 1) == jnp.bitwise_and(iota((rows, LANES), 0), 3)
    asked = jnp.where(own, asked, 0.0).astype(BF16)
    which = jnp.bitwise_and(iota((LANES, 512), 0), 1) == lax.shift_right_logical(iota((LANES, 512), 1), 8)
    both = mm(asked, ones_where(which))
    high_ref[...] = both[:, :256].astype(BF16)
    hot_ref[...] = ones_where(both[:, 256:] == iota((rows, 256), 1).astype(F32))

    def part(first, part_ref):
        hot = [
            jnp.where(high_ref[...] == jnp.array(first + k, BF16), hot_ref[...], jnp.zeros((), BF16))
            for k in range(part_ref.shape[0] // 256)
        ]
        return mm(jnp.concatenate(hot, axis=1), part_ref[...])

    acc_ref[...] = part(0, staged_ref)
    rest.wait()
    acc_ref[...] += part(staged // 256, rest_ref)
    quarter = [
        acc_ref[:, q * LANES : (q + 1) * LANES].reshape(rows // 8, 8, LANES) for q in range(width // LANES)
    ]
    first = iota((rows // 8, 8, LANES), 1) < 4

    def even(a, b):
        return jnp.where(first, a, pltpu.roll(b, 4, axis=1))

    def odd(a, b):
        return jnp.where(first, pltpu.roll(a, 4, axis=1), b)

    packed = jnp.concatenate(
        [
            even(quarter[0], quarter[1]),
            even(quarter[2], quarter[3]),
            odd(quarter[0], quarter[1]),
            odd(quarter[2], quarter[3]),
        ],
        axis=1,
    )
    out_ref[...] = packed.reshape(rows * 4, LANES).astype(BF16)


def attend_kernel(
    len_ref,
    slot_ref,
    answer_ref,
    history_ref,
    value_hbm_ref,
    click_hbm_ref,
    convert_hbm_ref,
    click_out_ref,
    convert_out_ref,
    rate_ref,
    both_ref,
    hist_ref,
    value_ref,
    click_ref,
    convert_ref,
    query_ref,
    joined_ref,
    acc_ref,
    max_ref,
    sum_ref,
    score_a_ref,
    score_b_ref,
    item_ref,
    hist_sem,
    weight_sem,
):
    users, seq, width = history_ref.shape
    cands = rate_ref.shape[1]
    head_width = width // HEADS
    total = users * cands
    pieces = seq // CHUNK

    def copy(u, j):
        part = pl.ds(j * CHUNK, CHUNK)
        return pltpu.make_async_copy(history_ref.at[u, part], hist_ref.at[u, part], hist_sem.at[u, j])

    weights = [
        pltpu.make_async_copy(source, target, weight_sem.at[k])
        for k, (source, target) in enumerate(
            ((value_hbm_ref, value_ref), (click_hbm_ref, click_ref), (convert_hbm_ref, convert_ref))
        )
    ]

    items = jnp.int32(0)
    for u in range(users):
        for j in range(pieces):

            @pl.when(len_ref[u] > j * CHUNK)
            def _():
                item_ref[items + j] = u * pieces + j
                copy(u, j).start()

        items += lax.div(len_ref[u] + (CHUNK - 1), CHUNK)
    for weight in weights:
        weight.start()

    group = answer_ref.shape[0] // 32
    got = answer_ref[...].astype(F32).reshape(group, 32, LANES)
    a0, b0, a1, b1 = (got[:, 8 * k : 8 * k + 8] for k in range(4))
    first = iota((group, 8, LANES), 1) < 4
    quarters = [
        jnp.where(first, a0, pltpu.roll(a1, 4, axis=1)),
        jnp.where(first, pltpu.roll(a0, 4, axis=1), a1),
        jnp.where(first, b0, pltpu.roll(b1, 4, axis=1)),
        jnp.where(first, pltpu.roll(b0, 4, axis=1), b1),
    ]
    answers = jnp.concatenate([q.reshape(group * 8, LANES).astype(BF16) for q in quarters], axis=1)
    place = jnp.transpose(slot_ref[...])[:, 0:1]
    pick = ones_where(place == iota((total, group * 8), 1).astype(F32))
    rows_got = mm(pick, answers)
    joined_ref[:, width:] = rows_got.astype(BF16)
    head_of_lane = lax.shift_right_logical(iota((cands, width), 1), head_width.bit_length() - 1)
    for u in range(users):
        target = rows_got[u * cands : (u + 1) * cands, :width] * (1.0 / math.sqrt(head_width))
        for h in range(HEADS):
            query_ref[u, h * cands : (h + 1) * cands, :] = jnp.where(
                head_of_lane == h, target, 0.0
            ).astype(BF16)

    acc_ref[...] = jnp.zeros(acc_ref.shape, F32)
    sum_ref[...] = jnp.zeros(sum_ref.shape, F32)
    max_ref[...] = jnp.full(max_ref.shape, NEG, F32)
    lane = iota((1, CHUNK), 1)

    def user_and_piece(i):
        item = item_ref[i]
        return lax.div(item, pieces), lax.rem(item, pieces)

    def arrive(i):
        @pl.when(i < items)
        def _():
            copy(*user_and_piece(i)).wait()

    def score(i, score_ref):
        u, j = user_and_piece(jnp.minimum(i, items - 1))
        scores = mm_nt(query_ref[u], hist_ref[u, pl.ds(j * CHUNK, CHUNK), :])
        scores = jnp.where(lane < len_ref[u] - j * CHUNK, scores, NEG)
        score_ref[...] = scores

    def gather(i, score_ref):
        u, j = user_and_piece(i)
        block = hist_ref[u, pl.ds(j * CHUNK, CHUNK), :]
        old = max_ref[u]
        new = jnp.maximum(old, jnp.max(score_ref[...], axis=1, keepdims=True))
        scale = jnp.exp(old - new)
        max_ref[u] = new
        added = sum_ref[u] * scale
        weight = []
        for k in range(CHUNK // LANES):
            w = jnp.exp(score_ref[:, k * LANES : (k + 1) * LANES] - new)
            added += w
            weight.append(w.astype(BF16))
        sum_ref[u] = added
        context = mm(jnp.concatenate(weight, axis=1), block)
        for k in range(width // LANES):
            part = slice(k * LANES, (k + 1) * LANES)
            acc_ref[u, :, part] = acc_ref[u, :, part] * scale + context[:, part]

    arrive(0)
    score(0, score_a_ref)

    def pair(p, carry):
        i = 2 * p
        arrive(i + 1)
        score(i + 1, score_b_ref)
        gather(i, score_a_ref)
        arrive(i + 2)

        @pl.when(i + 1 < items)
        def _():
            score(i + 2, score_a_ref)
            gather(i + 1, score_b_ref)

        return carry

    lax.fori_loop(0, lax.div(items + 1, 2), pair, 0)
    for weight in weights:
        weight.wait()

    row = iota((LANES, 1), 0)
    nothing = jnp.zeros((LANES, width), F32)
    click_out = jnp.where(row == 0, click_out_ref[...].astype(F32), nothing)
    convert_out = jnp.where(row == 1, convert_out_ref[...].astype(F32), nothing)
    out_weight = jnp.concatenate([click_out, convert_out], axis=1).astype(BF16)
    towers = (click_ref, convert_ref)
    early = [mm(joined_ref[:, width:], hidden[width:, :]) for hidden in towers]

    context = acc_ref[...].reshape(users * HEADS * cands, width)
    coarse = context.astype(BF16)
    fine = (context - coarse.astype(F32)).astype(BF16)
    number = mm(coarse, value_ref[...]) + mm(fine, value_ref[...])
    interest = []
    for u in range(users):
        above = jnp.zeros((cands, width), F32)
        below = jnp.ones((cands, width), F32)
        for h in range(HEADS):
            head = slice(h * cands, (h + 1) * cands)
            above = jnp.where(head_of_lane == h, number[u * HEADS * cands :][head], above)
            below = jnp.where(head_of_lane == h, jnp.sum(sum_ref[u, head], axis=1, keepdims=True), below)
        pooled = above / below
        square = jnp.mean(pooled * pooled, axis=1, keepdims=True)
        interest.append((pooled * lax.rsqrt(square + 1e-06)).astype(BF16))
    interest = jnp.concatenate(interest, axis=0)
    act = jnp.concatenate(
        [
            jnp.maximum(mm(interest, hidden[:width, :]) + part, 0.0).astype(BF16)
            for hidden, part in zip(towers, early)
        ],
        axis=1,
    )
    logit = jnp.transpose(mm_nt(act, out_weight))
    rate = jax.nn.sigmoid(logit[0:1])
    both = rate * jax.nn.sigmoid(logit[1:2])
    for u in range(users):
        rate_ref[u : u + 1, :] = rate[:, u * cands : (u + 1) * cands]
        both_ref[u : u + 1, :] = both[:, u * cands : (u + 1) * cands]


def stage_kernel(from_ref, to_ref, sem_ref):
    copy = pltpu.make_async_copy(from_ref.at[pl.ds(0, to_ref.shape[0])], to_ref, sem_ref)
    copy.start()
    copy.wait()


def stage(x, count):
    staged = pl.pallas_call(
        stage_kernel,
        out_shape=pltpu.VMEM((count,) + x.shape[1:], x.dtype),
        in_specs=[hbm()],
        out_specs=vmem(),
        scratch_shapes=[pltpu.SemaphoreType.DMA(())],
        cost_estimate=pl.CostEstimate(flops=1 << 30, bytes_accessed=2 * x.size, transcendentals=0),
        compiler_params=limit(2),
        name="stage",
    )(x)
    return pltpu.with_memory_space_constraint(staged, pltpu.VMEM)


def hbm():
    return pl.BlockSpec(memory_space=pltpu.HBM)


def limit(mib):
    return pltpu.CompilerParams(vmem_limit_bytes=mib << 20)


def vmem():
    return pl.BlockSpec(memory_space=pltpu.VMEM)


def local(
    history,
    lengths,
    candidates,
    item_table,
    value_weight,
    click_hidden,
    convert_hidden,
    click_output,
    convert_output,
):
    users, seq, width = history.shape
    cands = candidates.shape[1]
    table_rows, row_width = item_table.shape
    devices = lax.axis_size("gx") * lax.axis_size("gy")
    total = users * cands
    rows = HEADS * cands
    table = pltpu.with_memory_space_constraint(item_table, pltpu.HBM)
    staged = 5 * table_rows // 8

    request, place = pl.pallas_call(
        functools.partial(request_kernel, owners=devices, row_bits=table_rows.bit_length() - 1),
        out_shape=(pltpu.VMEM((devices, LANES), F32), pltpu.VMEM((8, total), F32)),
        in_specs=[vmem()],
        out_specs=(vmem(), vmem()),
        compiler_params=limit(8),
        name="request",
    )(candidates)
    asked = lax.all_to_all(request, AXES, 0, 0, tiled=True)
    answer = pl.pallas_call(
        answer_kernel,
        out_shape=jax.ShapeDtypeStruct((devices * 16, LANES), BF16),
        in_specs=[vmem(), vmem(), hbm()],
        out_specs=vmem(),
        scratch_shapes=[
            pltpu.VMEM((devices * SLOTS, 256), BF16),
            pltpu.VMEM((devices * SLOTS, 256), BF16),
            pltpu.VMEM((devices * SLOTS, row_width), F32),
            pltpu.VMEM((table_rows - staged, row_width), BF16),
            pltpu.SemaphoreType.DMA(()),
        ],
        compiler_params=limit(24),
        name="answer",
    )(asked, stage(table, staged), table)
    answered = lax.all_to_all(answer, AXES, 0, 0, tiled=True)
    return pl.pallas_call(
        attend_kernel,
        out_shape=(
            jax.ShapeDtypeStruct((users, cands), F32),
            jax.ShapeDtypeStruct((users, cands), F32),
        ),
        in_specs=[pl.BlockSpec(memory_space=pltpu.SMEM), vmem(), vmem(), hbm(), hbm(), hbm(), hbm(), vmem(), vmem()],
        out_specs=(vmem(), vmem()),
        scratch_shapes=[
            pltpu.VMEM((users, seq, width), BF16),
            pltpu.VMEM(value_weight.shape, BF16),
            pltpu.VMEM(click_hidden.shape, BF16),
            pltpu.VMEM(convert_hidden.shape, BF16),
            pltpu.VMEM((users, rows, width), BF16),
            pltpu.VMEM((total, 3 * width), BF16),
            pltpu.VMEM((users, rows, width), F32),
            pltpu.VMEM((users, rows, LANES), F32),
            pltpu.VMEM((users, rows, LANES), F32),
            pltpu.VMEM((rows, CHUNK), F32),
            pltpu.VMEM((rows, CHUNK), F32),
            pltpu.SMEM((users * (seq // CHUNK) + 1,), jnp.int32),
            pltpu.SemaphoreType.DMA((users, seq // CHUNK)),
            pltpu.SemaphoreType.DMA((3,)),
        ],
        compiler_params=limit(24),
        name="attend",
    )(
        lengths,
        place,
        answered,
        *(
            pltpu.with_memory_space_constraint(x, pltpu.HBM)
            for x in (history, value_weight, click_hidden, convert_hidden)
        ),
        click_output.reshape(1, -1),
        convert_output.reshape(1, -1),
    )


def solution(mesh):
    split = P(AXES)
    return jax.shard_map(
        local,
        mesh=mesh,
        in_specs=(split, split, split, split, P(), P(), P(), P(), P()),
        out_specs=(split, split),
        check_vma=False,
    )
```

profile of v0, /device:TPU:0, one launch (start us, length us, event | category | flops | bytes accessed | tf_op | source)
XLA Modules:
  0.0 51.1 jit_solution(533673935419008045)
XLA Ops:
  0.6 0.0 copy-start
  0.6 0.7 %copy-done = s32[4,64]{1,0:T(4,128)S(1)} copy-done((s32[4,64]{1,0:T(4,128)S(1)}, s32[4,64]{1,0:T(4,128)}, u32[]{:S(2)}) %copy-start) | copy-done | bytes 1048
  1.3 1.1 %request.1 = (f32[128,128]{1,0:T(8,128)}, f32[8,256]{1,0:T(8,128)S(1)}) custom-call(s32[4,64]{1,0:T(4,128)S(1)} %copy-done), custom_call_target="tpu_custom_call" | custom-call | tf_op jit(solution)/shard_map/request/pallas_call | solution.py:340
  2.4 11.2 %all-to-all-start = ((f32[128,1,128]{2,1,0:T(1,128)}), f32[128,1,128]{2,1,0:T(1,128)S(1)}, u32[]{:S(2)}, u32[]{:S(2)}) async-start(f32[128,1,128]{2,1,0:T(1,128)} %bitcast.1), calls=%async_computation | async-start | bytes 131072 | tf_op jit(solution)/shard_map/all_to_all | solution.py:348
  13.6 1.8 %stage.1.staged_ref = bf16[2560,512]{1,0:T(8,128)(2,1)S(1)} custom-call(bf16[4096,512]{1,0:T(8,128)(2,1)} %table_ref.1), custom_call_target="tpu_custom_call" | custom-call | flops 1073741824 | bytes 4194304 | tf_op jit(solution)/shard_map/stage/pallas_call | solution.py:295
  15.3 7.5 %all-to-all-done = f32[128,1,128]{2,1,0:T(1,128)S(1)} async-done(((f32[128,1,128]{2,1,0:T(1,128)}), f32[128,1,128]{2,1,0:T(1,128)S(1)}, u32[]{:S(2)}, u32[]{:S(2)}) %all-to-all-start) | async-done | bytes 65568 | tf_op jit(solution)/shard_map/all_to_all | solution.py:348
  22.9 0.0 copy-start.2
  22.9 0.0 copy-start.3
  22.9 0.0 copy-start.1
  22.9 3.4 %answer.1 = bf16[2048,128]{1,0:T(8,128)(2,1)} custom-call(f32[128,128]{1,0:T(8,128)S(1)} %bitcast.7, bf16[2560,512]{1,0:T(8,128)(2,1)S(1)} %stage.1.staged_ref, bf16[4096,512]{1,0:T(8,128)(2,1)} %table_ref.1), custom_call_target="tpu_custom_call" | custom-call | tf_op jit(solution)/shard_map/answer/pallas_call | solution.py:349
  26.3 4.8 %all-to-all-start.1 = ((bf16[128,16,128]{2,1,0:T(8,128)(2,1)}), bf16[128,16,128]{2,1,0:T(8,128)(2,1)S(1)}, u32[]{:S(2)}, u32[]{:S(2)}) async-start(bf16[128,16,128]{2,1,0:T(8,128)(2,1)} %bitcast.3), calls=%async_computation.1 | async-start | bytes 1048576 | tf_op jit(solution)/shard_map/all_to_all | solution.py:364
  31.1 0.0 copy-done.2
  31.2 0.0 copy-done.3
  31.2 13.5 %all-to-all-done.1 = bf16[128,16,128]{2,1,0:T(8,128)(2,1)S(1)} async-done(((bf16[128,16,128]{2,1,0:T(8,128)(2,1)}), bf16[128,16,128]{2,1,0:T(8,128)(2,1)S(1)}, u32[]{:S(2)}, u32[]{:S(2)}) %all-to-all-start.1) | async-done | bytes 524320 | tf_op jit(solution)/shard_map/all_to_all | solution.py:364
  44.6 0.0 copy-done.1
  44.7 6.5 %attend.1 = (f32[4,64]{1,0:T(4,128)}, f32[4,64]{1,0:T(4,128)}) custom-call(s32[4]{0:T(128)S(1)} %copy-done.1, f32[8,256]{1,0:T(8,128)S(1)} %get-tuple-element.4.slot_ref, bf16[2048,128]{1,0:T(8,128)(2,1)S(1)} %bitcast.6, bf16[4,2048,256]{2,1,0:T(8,128)(2,1)} %history_ref.1, bf16[256,256]{1,0:T(8,128)(2,1)} %value_hbm_ref.1, bf16[768,256]{1,0:T(8,128)(2,1)} %click_hbm_ref.1, ...), custom_call_target="tpu_custom_call" | custom-call | tf_op jit(solution)/shard_map/attend/pallas_call | solution.py:365
  (2 shorter events, 0.0 us)
Async XLA Ops:
  0.6 0.7 %copy-start = (s32[4,64]{1,0:T(4,128)S(1)}, s32[4,64]{1,0:T(4,128)}, u32[]{:S(2)}) copy-start(s32[4,64]{1,0:T(4,128)} %cand_ref.1) | copy-start | bytes 3076
  2.4 20.5 %all-to-all-start = ((f32[128,1,128]{2,1,0:T(1,128)}), f32[128,1,128]{2,1,0:T(1,128)S(1)}, u32[]{:S(2)}, u32[]{:S(2)}) async-start(f32[128,1,128]{2,1,0:T(1,128)} %bitcast.1), calls=%async_computation | async-start | bytes 131072 | tf_op jit(solution)/shard_map/all_to_all | solution.py:348
  22.9 8.3 %copy-start.2 = (bf16[256]{0:T(256)(128)(2,1)S(1)}, bf16[256]{0:T(256)(128)(2,1)}, u32[]{:S(2)}) copy-start(bf16[256]{0:T(256)(128)(2,1)} %param.16) | copy-start | bytes 1540
  22.9 8.3 %copy-start.3 = (bf16[256]{0:T(256)(128)(2,1)S(1)}, bf16[256]{0:T(256)(128)(2,1)}, u32[]{:S(2)}) copy-start(bf16[256]{0:T(256)(128)(2,1)} %param.17) | copy-start | bytes 1540
  22.9 21.8 %copy-start.1 = (s32[4]{0:T(128)S(1)}, s32[4]{0:T(128)}, u32[]{:S(2)}) copy-start(s32[4]{0:T(128)} %len_ref.1) | copy-start | bytes 52
  26.3 18.3 %all-to-all-start.1 = ((bf16[128,16,128]{2,1,0:T(8,128)(2,1)}), bf16[128,16,128]{2,1,0:T(8,128)(2,1)S(1)}, u32[]{:S(2)}, u32[]{:S(2)}) async-start(bf16[128,16,128]{2,1,0:T(8,128)(2,1)} %bitcast.3), calls=%async_computation.1 | async-start | bytes 1048576 | tf_op jit(solution)/shard_map/all_to_all | solution.py:364
where the time goes:
time: 51.7 us; the launch traced here: 51.1 us
  waiting for transfers between devices  21 us (41%)
  starting transfers between devices  16 us (31%)
  Pallas kernels  12.7 us (25%)
  local copies, waits for them, and re-layouts  0.7 us (1%)
  between operations  0.7 us (1%)
    all_to_all x1, waiting for transfers between devices, local(): answered = lax.all_to_all(answer, AXES, 0, 0, tiled=True)  13.5 us
    all_to_all x1, starting transfers between devices, local(): asked = lax.all_to_all(request, AXES, 0, 0, tiled=True)  11.2 us
    all_to_all x1, waiting for transfers between devices, local(): asked = lax.all_to_all(request, AXES, 0, 0, tiled=True)  7.54 us
    pallas_call x1, Pallas kernels, local(): pl.pallas_call(attend_kernel, out_shape=(jax.ShapeDtypeStruct((users, can...  6.46 us
    all_to_all x1, starting transfers between devices, local(): answered = lax.all_to_all(answer, AXES, 0, 0, tiled=True)  4.82 us
    pallas_call x1, Pallas kernels, local(): pl.pallas_call(answer_kernel, out_shape=jax.ShapeDtypeStruct((devices * 1...  3.44 us
    pallas_call x1, Pallas kernels, stage(): pl.pallas_call(stage_kernel, out_shape=pltpu.VMEM((count,) + x.shape[1:],...  1.75 us
    pallas_call x1, Pallas kernels, local(): pl.pallas_call(functools.partial(request_kernel, owners=devices, row_bits...  1.06 us
  transfers between devices with their start and end apart: 2, of which 2 were waited for; matrix products, arithmetic and copies ran while one was open for 0% of the time, Pallas kernels for 3%

commit v1 on v0

--- a/solution.py
+++ b/solution.py
@@ -107,21 +107,20 @@
 
 
 def attend_kernel(
-    len_ref,
-    slot_ref,
+    len_hbm_ref,
+    live_ref,
+    pick_ref,
     answer_ref,
+    last_ref,
+    value_ref,
+    click_ref,
+    convert_ref,
     history_ref,
-    value_hbm_ref,
-    click_hbm_ref,
-    convert_hbm_ref,
     click_out_ref,
     convert_out_ref,
     rate_ref,
     both_ref,
     hist_ref,
-    value_ref,
-    click_ref,
-    convert_ref,
     query_ref,
     joined_ref,
     acc_ref,
@@ -129,9 +128,15 @@
     sum_ref,
     score_a_ref,
     score_b_ref,
+    weight_a_ref,
+    weight_b_ref,
+    scale_a_ref,
+    scale_b_ref,
+    early_ref,
     item_ref,
+    len_ref,
     hist_sem,
-    weight_sem,
+    len_sem,
 ):
     users, seq, width = history_ref.shape
     cands = rate_ref.shape[1]
@@ -139,29 +144,12 @@
     total = users * cands
     pieces = seq // CHUNK
 
-    def copy(u, j):
-        part = pl.ds(j * CHUNK, CHUNK)
-        return pltpu.make_async_copy(history_ref.at[u, part], hist_ref.at[u, part], hist_sem.at[u, j])
-
-    weights = [
-        pltpu.make_async_copy(source, target, weight_sem.at[k])
-        for k, (source, target) in enumerate(
-            ((value_hbm_ref, value_ref), (click_hbm_ref, click_ref), (convert_hbm_ref, convert_ref))
-        )
-    ]
-
-    items = jnp.int32(0)
-    for u in range(users):
-        for j in range(pieces):
-
-            @pl.when(len_ref[u] > j * CHUNK)
-            def _():
-                item_ref[items + j] = u * pieces + j
-                copy(u, j).start()
-
-        items += lax.div(len_ref[u] + (CHUNK - 1), CHUNK)
-    for weight in weights:
-        weight.start()
+    def rest(u):
+        part = pl.ds(0, seq - CHUNK)
+        return pltpu.make_async_copy(history_ref.at[u, part], hist_ref.at[u], hist_sem.at[u])
+
+    lengths = pltpu.make_async_copy(len_hbm_ref, len_ref, len_sem)
+    lengths.start()
 
     group = answer_ref.shape[0] // 32
     got = answer_ref[...].astype(F32).reshape(group, 32, LANES)
@@ -174,9 +162,7 @@
         jnp.where(first, pltpu.roll(b0, 4, axis=1), b1),
     ]
     answers = jnp.concatenate([q.reshape(group * 8, LANES).astype(BF16) for q in quarters], axis=1)
-    place = jnp.transpose(slot_ref[...])[:, 0:1]
-    pick = ones_where(place == iota((total, group * 8), 1).astype(F32))
-    rows_got = mm(pick, answers)
+    rows_got = mm(pick_ref[...], answers)
     joined_ref[:, width:] = rows_got.astype(BF16)
     head_of_lane = lax.shift_right_logical(iota((cands, width), 1), head_width.bit_length() - 1)
     for u in range(users):
@@ -186,78 +172,105 @@
                 head_of_lane == h, target, 0.0
             ).astype(BF16)
 
-    acc_ref[...] = jnp.zeros(acc_ref.shape, F32)
-    sum_ref[...] = jnp.zeros(sum_ref.shape, F32)
-    max_ref[...] = jnp.full(max_ref.shape, NEG, F32)
+    lengths.wait()
+
+    def begin(u, carry):
+        @pl.when(len_ref[u] > CHUNK)
+        def _():
+            rest(u).start()
+
+        return carry
+
+    lax.fori_loop(0, users, begin, 0)
+
+    towers = (click_ref, convert_ref)
+    for k, hidden in enumerate(towers):
+        early_ref[k] = mm(joined_ref[:, width:], hidden[width:, :])
     lane = iota((1, CHUNK), 1)
 
-    def user_and_piece(i):
-        item = item_ref[i]
-        return lax.div(item, pieces), lax.rem(item, pieces)
-
-    def arrive(i):
-        @pl.when(i < items)
-        def _():
-            copy(*user_and_piece(i)).wait()
-
-    def score(i, score_ref):
-        u, j = user_and_piece(jnp.minimum(i, items - 1))
-        scores = mm_nt(query_ref[u], hist_ref[u, pl.ds(j * CHUNK, CHUNK), :])
-        scores = jnp.where(lane < len_ref[u] - j * CHUNK, scores, NEG)
-        score_ref[...] = scores
-
-    def gather(i, score_ref):
-        u, j = user_and_piece(i)
-        block = hist_ref[u, pl.ds(j * CHUNK, CHUNK), :]
+    def exp_parts(scores_of, top):
+        added = None
+        weight = []
+        for k in range(CHUNK // LANES):
+            w = jnp.exp(scores_of(slice(k * LANES, (k + 1) * LANES)) - top)
+            added = w if added is None else added + w
+            weight.append(w.astype(BF16))
+        return jnp.concatenate(weight, axis=1), added
+
+    for u in range(users):
+        block = last_ref[u]
+        live = jnp.concatenate([live_ref[u : u + 1, :]] * (CHUNK // LANES), axis=1)
+        scores = jnp.where(lane < live, mm_nt(query_ref[u], block), NEG)
+        top = jnp.broadcast_to(jnp.max(scores, axis=1, keepdims=True), (scores.shape[0], LANES))
+        max_ref[u] = top
+        weight, sum_ref[u] = exp_parts(lambda part: scores[:, part], top)
+        acc_ref[u] = mm(weight, block)
+
+    def enter(k, user, source, offset, wait):
+        for field, value in enumerate((user, source, offset, wait)):
+            item_ref[field, k] = value
+
+    items = jnp.int32(0)
+    for u in range(users):
+        for j in range(1, pieces):
+
+            @pl.when(len_ref[u] > j * CHUNK)
+            def _():
+                enter(items + (j + 1), u, u, (j - 1) * CHUNK, int(j == 1))
+
+        items += lax.div(len_ref[u] - 1, CHUNK)
+    for k in (0, 1, *(items + (k + 2) for k in range(5))):
+        enter(k, users, 0, 0, 0)
+
+    def entry(k):
+        return tuple(item_ref[field, k] for field in range(4))
+
+    def block(item):
+        return hist_ref[item[1], pl.ds(pl.multiple_of(item[2], CHUNK), CHUNK), :]
+
+    def step(now, ahead, beyond, score_to_ref, score_ref, weight_to_ref, scale_to_ref, weight_ref, scale_ref):
+        score_to_ref[...] = mm_nt(query_ref[beyond[1]], block(beyond))
+
+        u = ahead[0]
         old = max_ref[u]
         new = jnp.maximum(old, jnp.max(score_ref[...], axis=1, keepdims=True))
         scale = jnp.exp(old - new)
         max_ref[u] = new
-        added = sum_ref[u] * scale
-        weight = []
-        for k in range(CHUNK // LANES):
-            w = jnp.exp(score_ref[:, k * LANES : (k + 1) * LANES] - new)
-            added += w
-            weight.append(w.astype(BF16))
-        sum_ref[u] = added
-        context = mm(jnp.concatenate(weight, axis=1), block)
+        scale_to_ref[...] = scale
+        weight_to_ref[...], added = exp_parts(lambda part: score_ref[:, part], new)
+        sum_ref[u] = sum_ref[u] * scale + added
+
+        u = now[0]
+        context = mm(weight_ref[...], block(now))
+        scale = scale_ref[...]
         for k in range(width // LANES):
             part = slice(k * LANES, (k + 1) * LANES)
             acc_ref[u, :, part] = acc_ref[u, :, part] * scale + context[:, part]
 
-    arrive(0)
-    score(0, score_a_ref)
-
     def pair(p, carry):
-        i = 2 * p
-        arrive(i + 1)
-        score(i + 1, score_b_ref)
-        gather(i, score_a_ref)
-        arrive(i + 2)
-
-        @pl.when(i + 1 < items)
-        def _():
-            score(i + 2, score_a_ref)
-            gather(i + 1, score_b_ref)
-
-        return carry
-
-    lax.fori_loop(0, lax.div(items + 1, 2), pair, 0)
-    for weight in weights:
-        weight.wait()
+        a, b, c, d = carry
+        for item in (c, d):
+
+            @pl.when(item[3] == 1)
+            def _():
+                rest(item[1]).wait()
+
+        step(a, b, c, score_a_ref, score_b_ref, weight_b_ref, scale_b_ref, weight_a_ref, scale_a_ref)
+        step(b, c, d, score_b_ref, score_a_ref, weight_a_ref, scale_a_ref, weight_b_ref, scale_b_ref)
+        return c, d, entry(2 * p + 4), entry(2 * p + 5)
+
+    @pl.when(items > 0)
+    def _():
+        lax.fori_loop(0, lax.div(items + 3, 2), pair, tuple(entry(k) for k in range(4)))
 
     row = iota((LANES, 1), 0)
     nothing = jnp.zeros((LANES, width), F32)
     click_out = jnp.where(row == 0, click_out_ref[...].astype(F32), nothing)
     convert_out = jnp.where(row == 1, convert_out_ref[...].astype(F32), nothing)
     out_weight = jnp.concatenate([click_out, convert_out], axis=1).astype(BF16)
-    towers = (click_ref, convert_ref)
-    early = [mm(joined_ref[:, width:], hidden[width:, :]) for hidden in towers]
-
-    context = acc_ref[...].reshape(users * HEADS * cands, width)
-    coarse = context.astype(BF16)
-    fine = (context - coarse.astype(F32)).astype(BF16)
-    number = mm(coarse, value_ref[...]) + mm(fine, value_ref[...])
+
+    context = acc_ref[:users].reshape(users * HEADS * cands, width)
+    number = mm(context.astype(BF16), value_ref[...])
     interest = []
     for u in range(users):
         above = jnp.zeros((cands, width), F32)
@@ -272,8 +285,8 @@
     interest = jnp.concatenate(interest, axis=0)
     act = jnp.concatenate(
         [
-            jnp.maximum(mm(interest, hidden[:width, :]) + part, 0.0).astype(BF16)
-            for hidden, part in zip(towers, early)
+            jnp.maximum(mm(interest, hidden[:width, :]) + early_ref[k], 0.0).astype(BF16)
+            for k, hidden in enumerate(towers)
         ],
         axis=1,
     )
@@ -285,24 +298,50 @@
         both_ref[u : u + 1, :] = both[:, u * cands : (u + 1) * cands]
 
 
+def earlier_rows(length):
+    return lax.div(length - 1, CHUNK) * CHUNK
+
+
 def stage_kernel(from_ref, to_ref, sem_ref):
     copy = pltpu.make_async_copy(from_ref.at[pl.ds(0, to_ref.shape[0])], to_ref, sem_ref)
     copy.start()
     copy.wait()
 
 
-def stage(x, count):
-    staged = pl.pallas_call(
-        stage_kernel,
-        out_shape=pltpu.VMEM((count,) + x.shape[1:], x.dtype),
-        in_specs=[hbm()],
-        out_specs=vmem(),
-        scratch_shapes=[pltpu.SemaphoreType.DMA(())],
-        cost_estimate=pl.CostEstimate(flops=1 << 30, bytes_accessed=2 * x.size, transcendentals=0),
-        compiler_params=limit(2),
-        name="stage",
-    )(x)
-    return pltpu.with_memory_space_constraint(staged, pltpu.VMEM)
+def prepare_kernel(len_ref, slot_ref, history_ref, *refs):
+    weights, (live_ref, pick_ref, last_ref), targets, sem_ref = refs[:3], refs[3:6], refs[6:9], refs[9]
+    copies = [
+        pltpu.make_async_copy(
+            history_ref.at[u, pl.ds(pl.multiple_of(earlier_rows(len_ref[u]), CHUNK), CHUNK)],
+            last_ref.at[u],
+            sem_ref.at[u],
+        )
+        for u in range(history_ref.shape[0])
+    ]
+    copies += [
+        pltpu.make_async_copy(source, target, sem_ref.at[history_ref.shape[0] + k])
+        for k, (source, target) in enumerate(zip(weights, targets))
+    ]
+    for copy in copies:
+        copy.start()
+    for u in range(history_ref.shape[0]):
+        live_ref[u : u + 1, :] = jnp.full((1, LANES), len_ref[u] - earlier_rows(len_ref[u]), jnp.int32)
+    place = jnp.transpose(slot_ref[...])[:, 0:1]
+    pick_ref[...] = ones_where(place == iota(pick_ref.shape, 1).astype(F32))
+    for copy in copies:
+        copy.wait()
+
+
+def in_hbm(x):
+    return pltpu.with_memory_space_constraint(x, pltpu.HBM)
+
+
+def in_vmem(x):
+    return pltpu.with_memory_space_constraint(x, pltpu.VMEM)
+
+
+def window_cost(size):
+    return pl.CostEstimate(flops=1 << 30, bytes_accessed=size, transcendentals=0)
 
 
 def hbm():
@@ -334,9 +373,21 @@
     devices = lax.axis_size("gx") * lax.axis_size("gy")
     total = users * cands
     rows = HEADS * cands
-    table = pltpu.with_memory_space_constraint(item_table, pltpu.HBM)
     staged = 5 * table_rows // 8
-
+    table = in_hbm(item_table)
+    history = in_hbm(history)
+    weights = (in_hbm(value_weight), in_hbm(click_hidden), in_hbm(convert_hidden))
+
+    table_start = pl.pallas_call(
+        stage_kernel,
+        out_shape=pltpu.VMEM((staged, row_width), BF16),
+        in_specs=[hbm()],
+        out_specs=vmem(),
+        scratch_shapes=[pltpu.SemaphoreType.DMA(())],
+        cost_estimate=window_cost(2 * table.size),
+        compiler_params=limit(2),
+        name="stage",
+    )(table)
     request, place = pl.pallas_call(
         functools.partial(request_kernel, owners=devices, row_bits=table_rows.bit_length() - 1),
         out_shape=(pltpu.VMEM((devices, LANES), F32), pltpu.VMEM((8, total), F32)),
@@ -360,42 +411,58 @@
         ],
         compiler_params=limit(24),
         name="answer",
-    )(asked, stage(table, staged), table)
+    )(asked, in_vmem(table_start), table)
     answered = lax.all_to_all(answer, AXES, 0, 0, tiled=True)
+    prepared = pl.pallas_call(
+        prepare_kernel,
+        out_shape=(
+            pltpu.VMEM((users, LANES), jnp.int32),
+            pltpu.VMEM((total, devices * SLOTS), BF16),
+            pltpu.VMEM((users, CHUNK, width), BF16),
+            *(pltpu.VMEM(w.shape, BF16) for w in weights),
+        ),
+        in_specs=[pl.BlockSpec(memory_space=pltpu.SMEM), vmem()] + [hbm()] * 4,
+        out_specs=(vmem(),) * 6,
+        scratch_shapes=[pltpu.SemaphoreType.DMA((users + 3,))],
+        cost_estimate=window_cost(1 << 22),
+        compiler_params=limit(4),
+        name="prepare",
+    )(lengths, place, history, *weights)
+    live, pick, start, *weights = (in_vmem(x) for x in prepared)
     return pl.pallas_call(
         attend_kernel,
         out_shape=(
             jax.ShapeDtypeStruct((users, cands), F32),
             jax.ShapeDtypeStruct((users, cands), F32),
         ),
-        in_specs=[pl.BlockSpec(memory_space=pltpu.SMEM), vmem(), vmem(), hbm(), hbm(), hbm(), hbm(), vmem(), vmem()],
+        in_specs=[hbm()] + [vmem()] * 7 + [hbm()] + [vmem()] * 2,
         out_specs=(vmem(), vmem()),
         scratch_shapes=[
-            pltpu.VMEM((users, seq, width), BF16),
-            pltpu.VMEM(value_weight.shape, BF16),
-            pltpu.VMEM(click_hidden.shape, BF16),
-            pltpu.VMEM(convert_hidden.shape, BF16),
+            pltpu.VMEM((users, seq - CHUNK, width), BF16),
             pltpu.VMEM((users, rows, width), BF16),
             pltpu.VMEM((total, 3 * width), BF16),
-            pltpu.VMEM((users, rows, width), F32),
-            pltpu.VMEM((users, rows, LANES), F32),
-            pltpu.VMEM((users, rows, LANES), F32),
-            pltpu.VMEM((rows, CHUNK), F32),
-            pltpu.VMEM((rows, CHUNK), F32),
-            pltpu.SMEM((users * (seq // CHUNK) + 1,), jnp.int32),
-            pltpu.SemaphoreType.DMA((users, seq // CHUNK)),
-            pltpu.SemaphoreType.DMA((3,)),
+            pltpu.VMEM((users + 1, rows, width), F32),
+            pltpu.VMEM((users + 1, rows, LANES), F32),
+            pltpu.VMEM((users + 1, rows, LANES), F32),
+            *[pltpu.VMEM((rows, CHUNK), F32)] * 2,
+            *[pltpu.VMEM((rows, CHUNK), BF16)] * 2,
+            *[pltpu.VMEM((rows, LANES), F32)] * 2,
+            pltpu.VMEM((2, total, click_hidden.shape[1]), F32),
+            pltpu.SMEM((4, users * (seq // CHUNK - 1) + 7), jnp.int32),
+            pltpu.SMEM((users,), jnp.int32),
+            pltpu.SemaphoreType.DMA((users,)),
+            pltpu.SemaphoreType.DMA(()),
         ],
         compiler_params=limit(24),
         name="attend",
     )(
-        lengths,
-        place,
+        in_hbm(lengths),
+        live,
+        pick,
         answered,
-        *(
-            pltpu.with_memory_space_constraint(x, pltpu.HBM)
-            for x in (history, value_weight, click_hidden, convert_hidden)
-        ),
+        start,
+        *weights,
+        history,
         click_output.reshape(1, -1),
         convert_output.reshape(1, -1),
     )

time: 51.7 us -> 50.6 us (0.979)
  waiting for transfers between devices: 21 us -> 18.9 us
  Pallas kernels: 12.7 us -> 13.3 us
    all_to_all x1, waiting for transfers between devices: 13.5 us -> 11.4 us  [local(): answered = lax.all_to_all(answer, AXES, 0, 0, tiled=True)]
    pallas_call x1 -> x2, Pallas kernels: 1.75 us -> 3.84 us  [the longest x1 2.09 us: local(): pl.pallas_call(prepare_kernel, out_shape=(pltpu.VMEM((users, LANES), jnp....]
    pallas_call x1, Pallas kernels: 6.46 us -> 4.94 us  [local(): pl.pallas_call(attend_kernel, out_shape=(jax.ShapeDtypeStruct((users, can...]
  transfers between devices with their start and end apart: 2 -> 2, of which waited for: 2 -> 2; matrix products, arithmetic and copies ran while one was open for 0% -> 0% of each run, Pallas kernels for 3% -> 8%
where the time goes in v1:
time: 50.6 us; the launch traced here: 49.6 us
  waiting for transfers between devices  18.9 us (37%)
  starting transfers between devices  16 us (32%)
  Pallas kernels  13.3 us (26%)
  between operations  0.72 us (1%)
  local copies, waits for them, and re-layouts  0.7 us (1%)
    all_to_all x1, waiting for transfers between devices, local(): answered = lax.all_to_all(answer, AXES, 0, 0, tiled=True)  11.4 us
    all_to_all x1, starting transfers between devices, local(): asked = lax.all_to_all(request, AXES, 0, 0, tiled=True)  11.2 us
    all_to_all x1, waiting for transfers between devices, local(): asked = lax.all_to_all(request, AXES, 0, 0, tiled=True)  7.56 us
    pallas_call x1, Pallas kernels, local(): pl.pallas_call(attend_kernel, out_shape=(jax.ShapeDtypeStruct((users, can...  4.94 us
    all_to_all x1, starting transfers between devices, local(): answered = lax.all_to_all(answer, AXES, 0, 0, tiled=True)  4.82 us
    pallas_call x1, Pallas kernels, local(): pl.pallas_call(answer_kernel, out_shape=jax.ShapeDtypeStruct((devices * 1...  3.44 us
    pallas_call x1, Pallas kernels, local(): pl.pallas_call(prepare_kernel, out_shape=(pltpu.VMEM((users, LANES), jnp....  2.09 us
    pallas_call x1, Pallas kernels, local(): pl.pallas_call(stage_kernel, out_shape=pltpu.VMEM((staged, row_width), BF...  1.75 us
  transfers between devices with their start and end apart: 2, of which 2 were waited for; matrix products, arithmetic and copies ran while one was open for 0% of the time, Pallas kernels for 8%

profile of v1, /device:TPU:0, one launch (start us, length us, event | category | flops | bytes accessed | tf_op | source)
XLA Modules:
  0.0 49.6 jit_solution(3034731412206539966)
XLA Ops:
  0.6 0.0 copy-start
  0.6 0.7 %copy-done = s32[4,64]{1,0:T(4,128)S(1)} copy-done((s32[4,64]{1,0:T(4,128)S(1)}, s32[4,64]{1,0:T(4,128)}, u32[]{:S(2)}) %copy-start) | copy-done | bytes 1048
  1.3 1.1 %request.1 = (f32[128,128]{1,0:T(8,128)}, f32[8,256]{1,0:T(8,128)S(1)}) custom-call(s32[4,64]{1,0:T(4,128)S(1)} %copy-done), custom_call_target="tpu_custom_call" | custom-call | tf_op jit(solution)/shard_map/request/pallas_call | solution.py:391
  2.4 11.2 %all-to-all-start = ((f32[128,1,128]{2,1,0:T(1,128)}), f32[128,1,128]{2,1,0:T(1,128)S(1)}, u32[]{:S(2)}, u32[]{:S(2)}) async-start(f32[128,1,128]{2,1,0:T(1,128)} %bitcast.1), calls=%async_computation | async-start | bytes 131072 | tf_op jit(solution)/shard_map/all_to_all | solution.py:399
  13.5 1.8 %stage.1.staged_ref = bf16[2560,512]{1,0:T(8,128)(2,1)S(1)} custom-call(bf16[4096,512]{1,0:T(8,128)(2,1)} %table_ref.1), custom_call_target="tpu_custom_call" | custom-call | flops 1073741824 | bytes 4194304 | tf_op jit(solution)/shard_map/stage/pallas_call | solution.py:381
  15.3 7.6 %all-to-all-done = f32[128,1,128]{2,1,0:T(1,128)S(1)} async-done(((f32[128,1,128]{2,1,0:T(1,128)}), f32[128,1,128]{2,1,0:T(1,128)S(1)}, u32[]{:S(2)}, u32[]{:S(2)}) %all-to-all-start) | async-done | bytes 65568 | tf_op jit(solution)/shard_map/all_to_all | solution.py:399
  22.9 0.0 copy-start.2
  22.9 0.0 copy-start.3
  22.9 0.0 copy-start.1
  22.9 3.4 %answer.1 = bf16[2048,128]{1,0:T(8,128)(2,1)} custom-call(f32[128,128]{1,0:T(8,128)S(1)} %bitcast.7, bf16[2560,512]{1,0:T(8,128)(2,1)S(1)} %stage.1.staged_ref, bf16[4096,512]{1,0:T(8,128)(2,1)} %table_ref.1), custom_call_target="tpu_custom_call" | custom-call | tf_op jit(solution)/shard_map/answer/pallas_call | solution.py:400
  26.3 4.8 %all-to-all-start.1 = ((bf16[128,16,128]{2,1,0:T(8,128)(2,1)}), bf16[128,16,128]{2,1,0:T(8,128)(2,1)S(1)}, u32[]{:S(2)}, u32[]{:S(2)}) async-start(bf16[128,16,128]{2,1,0:T(8,128)(2,1)} %bitcast.3), calls=%async_computation.1 | async-start | bytes 1048576 | tf_op jit(solution)/shard_map/all_to_all | solution.py:415
  31.1 0.0 copy-done.2
  31.2 0.0 copy-done.3
  31.2 0.0 copy-done.1
  31.2 2.1 %prepare.1 = (s32[4,128]{1,0:T(4,128)S(1)}, bf16[256,512]{1,0:T(8,128)(2,1)S(1)}, bf16[4,512,256]{2,1,0:T(8,128)(2,1)S(1)}, bf16[256,256]{1,0:T(8,128)(2,1)S(1)}...) custom-call(s32[4]{0:T(128)S(1)} %copy-done.1, f32[8,256]{1,0:T(8,128)S(1)} %get-tuple-element.10.slot_ref, ...), custom_call_target="tpu_custom_call" | custom-call | flops 1073741824 | bytes 4194304 | tf_op jit(solution)/shard_map/prepare/pallas_call | solution.py:416
  33.3 11.4 %all-to-all-done.1 = bf16[128,16,128]{2,1,0:T(8,128)(2,1)S(1)} async-done(((bf16[128,16,128]{2,1,0:T(8,128)(2,1)}), bf16[128,16,128]{2,1,0:T(8,128)(2,1)S(1)}, u32[]{:S(2)}, u32[]{:S(2)}) %all-to-all-start.1) | async-done | bytes 524320 | tf_op jit(solution)/shard_map/all_to_all | solution.py:415
  44.6 4.9 %attend.1 = (f32[4,64]{1,0:T(4,128)}, f32[4,64]{1,0:T(4,128)}) custom-call(s32[4]{0:T(128)} %len_hbm_ref.1, s32[4,128]{1,0:T(4,128)S(1)} %get-tuple-element.11.live_ref, bf16[256,512]{1,0:T(8,128)(2,1)S(1)} %get-tuple-element.12.pick_ref, bf16[2048,128]{1,0:T(8,128)(2,1)S(1)} %bitcast.6, bf16[4,512,256]{2,1,0:T(8,128)(2,1)S(1)} %get-tuple-element.14.last_ref, ...), custom_call_target="tpu_custom_call" | custom-call | tf_op jit(solution)/shard_map/attend/pallas_call | solution.py:432
  (2 shorter events, 0.0 us)
Async XLA Ops:
  0.6 0.7 %copy-start = (s32[4,64]{1,0:T(4,128)S(1)}, s32[4,64]{1,0:T(4,128)}, u32[]{:S(2)}) copy-start(s32[4,64]{1,0:T(4,128)} %cand_ref.1) | copy-start | bytes 3076
  2.4 20.5 %all-to-all-start = ((f32[128,1,128]{2,1,0:T(1,128)}), f32[128,1,128]{2,1,0:T(1,128)S(1)}, u32[]{:S(2)}, u32[]{:S(2)}) async-start(f32[128,1,128]{2,1,0:T(1,128)} %bitcast.1), calls=%async_computation | async-start | bytes 131072 | tf_op jit(solution)/shard_map/all_to_all | solution.py:399
  22.9 8.3 %copy-start.2 = (bf16[256]{0:T(256)(128)(2,1)S(1)}, bf16[256]{0:T(256)(128)(2,1)}, u32[]{:S(2)}) copy-start(bf16[256]{0:T(256)(128)(2,1)} %param.16) | copy-start | bytes 1540
  22.9 8.3 %copy-start.3 = (bf16[256]{0:T(256)(128)(2,1)S(1)}, bf16[256]{0:T(256)(128)(2,1)}, u32[]{:S(2)}) copy-start(bf16[256]{0:T(256)(128)(2,1)} %param.17) | copy-start | bytes 1540
  22.9 8.3 %copy-start.1 = (s32[4]{0:T(128)S(1)}, s32[4]{0:T(128)}, u32[]{:S(2)}) copy-start(s32[4]{0:T(128)} %len_hbm_ref.1) | copy-start | bytes 52
  26.3 18.3 %all-to-all-start.1 = ((bf16[128,16,128]{2,1,0:T(8,128)(2,1)}), bf16[128,16,128]{2,1,0:T(8,128)(2,1)S(1)}, u32[]{:S(2)}, u32[]{:S(2)}) async-start(bf16[128,16,128]{2,1,0:T(8,128)(2,1)} %bitcast.3), calls=%async_computation.1 | async-start | bytes 1048576 | tf_op jit(solution)/shard_map/all_to_all | solution.py:415

commit v2 on v1

--- a/solution.py
+++ b/solution.py
@@ -107,7 +107,6 @@
 
 
 def attend_kernel(
-    len_hbm_ref,
     live_ref,
     pick_ref,
     answer_ref,
@@ -136,7 +135,6 @@
     item_ref,
     len_ref,
     hist_sem,
-    len_sem,
 ):
     users, seq, width = history_ref.shape
     cands = rate_ref.shape[1]
@@ -148,8 +146,8 @@
         part = pl.ds(0, seq - CHUNK)
         return pltpu.make_async_copy(history_ref.at[u, part], hist_ref.at[u], hist_sem.at[u])
 
-    lengths = pltpu.make_async_copy(len_hbm_ref, len_ref, len_sem)
-    lengths.start()
+    for u in range(users):
+        len_ref[u] = jnp.max(live_ref[users + u : users + u + 1, :]).astype(jnp.int32)
 
     group = answer_ref.shape[0] // 32
     got = answer_ref[...].astype(F32).reshape(group, 32, LANES)
@@ -172,7 +170,6 @@
                 head_of_lane == h, target, 0.0
             ).astype(BF16)
 
-    lengths.wait()
 
     def begin(u, carry):
         @pl.when(len_ref[u] > CHUNK)
@@ -200,7 +197,7 @@
     for u in range(users):
         block = last_ref[u]
         live = jnp.concatenate([live_ref[u : u + 1, :]] * (CHUNK // LANES), axis=1)
-        scores = jnp.where(lane < live, mm_nt(query_ref[u], block), NEG)
+        scores = jnp.where(lane.astype(F32) < live, mm_nt(query_ref[u], block), NEG)
         top = jnp.broadcast_to(jnp.max(scores, axis=1, keepdims=True), (scores.shape[0], LANES))
         max_ref[u] = top
         weight, sum_ref[u] = exp_parts(lambda part: scores[:, part], top)
@@ -269,27 +266,35 @@
     convert_out = jnp.where(row == 1, convert_out_ref[...].astype(F32), nothing)
     out_weight = jnp.concatenate([click_out, convert_out], axis=1).astype(BF16)
 
-    context = acc_ref[:users].reshape(users * HEADS * cands, width)
-    number = mm(context.astype(BF16), value_ref[...])
     interest = []
     for u in range(users):
+        context = acc_ref[u]
+        coarse = context.astype(BF16)
+        fine = (context - coarse.astype(F32)).astype(BF16)
+        number = mm(coarse, value_ref[...]) + mm(fine, value_ref[...])
         above = jnp.zeros((cands, width), F32)
         below = jnp.ones((cands, width), F32)
         for h in range(HEADS):
             head = slice(h * cands, (h + 1) * cands)
-            above = jnp.where(head_of_lane == h, number[u * HEADS * cands :][head], above)
+            above = jnp.where(head_of_lane == h, number[head], above)
             below = jnp.where(head_of_lane == h, jnp.sum(sum_ref[u, head], axis=1, keepdims=True), below)
         pooled = above / below
         square = jnp.mean(pooled * pooled, axis=1, keepdims=True)
         interest.append((pooled * lax.rsqrt(square + 1e-06)).astype(BF16))
-    interest = jnp.concatenate(interest, axis=0)
-    act = jnp.concatenate(
-        [
-            jnp.maximum(mm(interest, hidden[:width, :]) + early_ref[k], 0.0).astype(BF16)
-            for k, hidden in enumerate(towers)
-        ],
-        axis=1,
-    )
+    act = []
+    for u in range(0, users, 4):
+        part = slice(u * cands, (u + 4) * cands)
+        query = jnp.concatenate(interest[u : u + 4], axis=0)
+        act.append(
+            jnp.concatenate(
+                [
+                    jnp.maximum(mm(query, hidden[:width, :]) + early_ref[k, part], 0.0).astype(BF16)
+                    for k, hidden in enumerate(towers)
+                ],
+                axis=1,
+            )
+        )
+    act = jnp.concatenate(act, axis=0)
     logit = jnp.transpose(mm_nt(act, out_weight))
     rate = jax.nn.sigmoid(logit[0:1])
     both = rate * jax.nn.sigmoid(logit[1:2])
@@ -324,8 +329,11 @@
     ]
     for copy in copies:
         copy.start()
-    for u in range(history_ref.shape[0]):
-        live_ref[u : u + 1, :] = jnp.full((1, LANES), len_ref[u] - earlier_rows(len_ref[u]), jnp.int32)
+    users = history_ref.shape[0]
+    for u in range(users):
+        live = len_ref[u] - earlier_rows(len_ref[u])
+        live_ref[u : u + 1, :] = jnp.full((1, LANES), live, jnp.int32).astype(F32)
+        live_ref[users + u : users + u + 1, :] = jnp.full((1, LANES), len_ref[u], jnp.int32).astype(F32)
     place = jnp.transpose(slot_ref[...])[:, 0:1]
     pick_ref[...] = ones_where(place == iota(pick_ref.shape, 1).astype(F32))
     for copy in copies:
@@ -416,7 +424,7 @@
     prepared = pl.pallas_call(
         prepare_kernel,
         out_shape=(
-            pltpu.VMEM((users, LANES), jnp.int32),
+            pltpu.VMEM((2 * users, LANES), F32),
             pltpu.VMEM((total, devices * SLOTS), BF16),
             pltpu.VMEM((users, CHUNK, width), BF16),
             *(pltpu.VMEM(w.shape, BF16) for w in weights),
@@ -435,7 +443,7 @@
             jax.ShapeDtypeStruct((users, cands), F32),
             jax.ShapeDtypeStruct((users, cands), F32),
         ),
-        in_specs=[hbm()] + [vmem()] * 7 + [hbm()] + [vmem()] * 2,
+        in_specs=[vmem()] * 7 + [hbm()] + [vmem()] * 2,
         out_specs=(vmem(), vmem()),
         scratch_shapes=[
             pltpu.VMEM((users, seq - CHUNK, width), BF16),
@@ -451,12 +459,10 @@
             pltpu.SMEM((4, users * (seq // CHUNK - 1) + 7), jnp.int32),
             pltpu.SMEM((users,), jnp.int32),
             pltpu.SemaphoreType.DMA((users,)),
-            pltpu.SemaphoreType.DMA(()),
         ],
         compiler_params=limit(24),
         name="attend",
     )(
-        in_hbm(lengths),
         live,
         pick,
         answered,

time: 50.6 us -> 50 us (0.988)
  no operation moved by 1% of the time
where the time goes in v2:
time: 50 us; the launch traced here: 49.4 us
  waiting for transfers between devices  18.9 us (38%)
  starting transfers between devices  16 us (32%)
  Pallas kernels  13.1 us (26%)
  between operations  0.72 us (1%)
  local copies, waits for them, and re-layouts  0.7 us (1%)
    all_to_all x1, waiting for transfers between devices, local(): answered = lax.all_to_all(answer, AXES, 0, 0, tiled=True)  11.4 us
    all_to_all x1, starting transfers between devices, local(): asked = lax.all_to_all(request, AXES, 0, 0, tiled=True)  11.2 us
    all_to_all x1, waiting for transfers between devices, local(): asked = lax.all_to_all(request, AXES, 0, 0, tiled=True)  7.56 us
    all_to_all x1, starting transfers between devices, local(): answered = lax.all_to_all(answer, AXES, 0, 0, tiled=True)  4.82 us
    pallas_call x1, Pallas kernels, local(): pl.pallas_call(attend_kernel, out_shape=(jax.ShapeDtypeStruct((users, can...  4.73 us
    pallas_call x1, Pallas kernels, local(): pl.pallas_call(answer_kernel, out_shape=jax.ShapeDtypeStruct((devices * 1...  3.44 us
    pallas_call x1, Pallas kernels, local(): pl.pallas_call(prepare_kernel, out_shape=(pltpu.VMEM((2 * users, LANES),...  2.09 us
    pallas_call x1, Pallas kernels, local(): pl.pallas_call(stage_kernel, out_shape=pltpu.VMEM((staged, row_width), BF...  1.75 us
  transfers between devices with their start and end apart: 2, of which 2 were waited for; matrix products, arithmetic and copies ran while one was open for 0% of the time, Pallas kernels for 8%

profile of v2, /device:TPU:0, one launch (start us, length us, event | category | flops | bytes accessed | tf_op | source)
XLA Modules:
  0.0 49.4 jit_solution(1899636316399885226)
XLA Ops:
  0.6 0.0 copy-start
  0.6 0.7 %copy-done = s32[4,64]{1,0:T(4,128)S(1)} copy-done((s32[4,64]{1,0:T(4,128)S(1)}, s32[4,64]{1,0:T(4,128)}, u32[]{:S(2)}) %copy-start) | copy-done | bytes 1048
  1.3 1.1 %request.1 = (f32[128,128]{1,0:T(8,128)}, f32[8,256]{1,0:T(8,128)S(1)}) custom-call(s32[4,64]{1,0:T(4,128)S(1)} %copy-done), custom_call_target="tpu_custom_call" | custom-call | tf_op jit(solution)/shard_map/request/pallas_call | solution.py:399
  2.4 11.2 %all-to-all-start = ((f32[128,1,128]{2,1,0:T(1,128)}), f32[128,1,128]{2,1,0:T(1,128)S(1)}, u32[]{:S(2)}, u32[]{:S(2)}) async-start(f32[128,1,128]{2,1,0:T(1,128)} %bitcast.1), calls=%async_computation | async-start | bytes 131072 | tf_op jit(solution)/shard_map/all_to_all | solution.py:407
  13.5 1.8 %stage.1.staged_ref = bf16[2560,512]{1,0:T(8,128)(2,1)S(1)} custom-call(bf16[4096,512]{1,0:T(8,128)(2,1)} %table_ref.1), custom_call_target="tpu_custom_call" | custom-call | flops 1073741824 | bytes 4194304 | tf_op jit(solution)/shard_map/stage/pallas_call | solution.py:389
  15.3 7.6 %all-to-all-done = f32[128,1,128]{2,1,0:T(1,128)S(1)} async-done(((f32[128,1,128]{2,1,0:T(1,128)}), f32[128,1,128]{2,1,0:T(1,128)S(1)}, u32[]{:S(2)}, u32[]{:S(2)}) %all-to-all-start) | async-done | bytes 65568 | tf_op jit(solution)/shard_map/all_to_all | solution.py:407
  22.9 0.0 copy-start.2
  22.9 0.0 copy-start.3
  22.9 0.0 copy-start.1
  22.9 3.4 %answer.1 = bf16[2048,128]{1,0:T(8,128)(2,1)} custom-call(f32[128,128]{1,0:T(8,128)S(1)} %bitcast.7, bf16[2560,512]{1,0:T(8,128)(2,1)S(1)} %stage.1.staged_ref, bf16[4096,512]{1,0:T(8,128)(2,1)} %table_ref.1), custom_call_target="tpu_custom_call" | custom-call | tf_op jit(solution)/shard_map/answer/pallas_call | solution.py:408
  26.3 4.8 %all-to-all-start.1 = ((bf16[128,16,128]{2,1,0:T(8,128)(2,1)}), bf16[128,16,128]{2,1,0:T(8,128)(2,1)S(1)}, u32[]{:S(2)}, u32[]{:S(2)}) async-start(bf16[128,16,128]{2,1,0:T(8,128)(2,1)} %bitcast.3), calls=%async_computation.1 | async-start | bytes 1048576 | tf_op jit(solution)/shard_map/all_to_all | solution.py:423
  31.1 0.0 copy-done.2
  31.2 0.0 copy-done.3
  31.2 0.0 copy-done.1
  31.2 2.1 %prepare.1 = (f32[8,128]{1,0:T(8,128)S(1)}, bf16[256,512]{1,0:T(8,128)(2,1)S(1)}, bf16[4,512,256]{2,1,0:T(8,128)(2,1)S(1)}, bf16[256,256]{1,0:T(8,128)(2,1)S(1)}...) custom-call(s32[4]{0:T(128)S(1)} %copy-done.1, f32[8,256]{1,0:T(8,128)S(1)} %get-tuple-element.10.slot_ref, ...), custom_call_target="tpu_custom_call" | custom-call | flops 1073741824 | bytes 4194304 | tf_op jit(solution)/shard_map/prepare/pallas_call | solution.py:424
  33.3 11.4 %all-to-all-done.1 = bf16[128,16,128]{2,1,0:T(8,128)(2,1)S(1)} async-done(((bf16[128,16,128]{2,1,0:T(8,128)(2,1)}), bf16[128,16,128]{2,1,0:T(8,128)(2,1)S(1)}, u32[]{:S(2)}, u32[]{:S(2)}) %all-to-all-start.1) | async-done | bytes 524320 | tf_op jit(solution)/shard_map/all_to_all | solution.py:423
  44.6 4.7 %attend.1 = (f32[4,64]{1,0:T(4,128)}, f32[4,64]{1,0:T(4,128)}) custom-call(f32[8,128]{1,0:T(8,128)S(1)} %get-tuple-element.11.live_ref, bf16[256,512]{1,0:T(8,128)(2,1)S(1)} %get-tuple-element.12.pick_ref, bf16[2048,128]{1,0:T(8,128)(2,1)S(1)} %bitcast.6, bf16[4,512,256]{2,1,0:T(8,128)(2,1)S(1)} %get-tuple-element.14.last_ref, ...), custom_call_target="tpu_custom_call" | custom-call | tf_op jit(solution)/shard_map/attend/pallas_call | solution.py:440
  (2 shorter events, 0.0 us)
Async XLA Ops:
  0.6 0.7 %copy-start = (s32[4,64]{1,0:T(4,128)S(1)}, s32[4,64]{1,0:T(4,128)}, u32[]{:S(2)}) copy-start(s32[4,64]{1,0:T(4,128)} %cand_ref.1) | copy-start | bytes 3076
  2.4 20.5 %all-to-all-start = ((f32[128,1,128]{2,1,0:T(1,128)}), f32[128,1,128]{2,1,0:T(1,128)S(1)}, u32[]{:S(2)}, u32[]{:S(2)}) async-start(f32[128,1,128]{2,1,0:T(1,128)} %bitcast.1), calls=%async_computation | async-start | bytes 131072 | tf_op jit(solution)/shard_map/all_to_all | solution.py:407
  22.9 8.3 %copy-start.2 = (bf16[256]{0:T(256)(128)(2,1)S(1)}, bf16[256]{0:T(256)(128)(2,1)}, u32[]{:S(2)}) copy-start(bf16[256]{0:T(256)(128)(2,1)} %param.16) | copy-start | bytes 1540
  22.9 8.3 %copy-start.3 = (bf16[256]{0:T(256)(128)(2,1)S(1)}, bf16[256]{0:T(256)(128)(2,1)}, u32[]{:S(2)}) copy-start(bf16[256]{0:T(256)(128)(2,1)} %param.17) | copy-start | bytes 1540
  22.9 8.3 %copy-start.1 = (s32[4]{0:T(128)S(1)}, s32[4]{0:T(128)}, u32[]{:S(2)}) copy-start(s32[4]{0:T(128)} %len_ref.1) | copy-start | bytes 52
  26.3 18.3 %all-to-all-start.1 = ((bf16[128,16,128]{2,1,0:T(8,128)(2,1)}), bf16[128,16,128]{2,1,0:T(8,128)(2,1)S(1)}, u32[]{:S(2)}, u32[]{:S(2)}) async-start(bf16[128,16,128]{2,1,0:T(8,128)(2,1)} %bitcast.3), calls=%async_computation.1 | async-start | bytes 1048576 | tf_op jit(solution)/shard_map/all_to_all | solution.py:423

commit v3 on v2

--- a/solution.py
+++ b/solution.py
@@ -132,6 +132,7 @@
     scale_a_ref,
     scale_b_ref,
     early_ref,
+    last_score_ref,
     item_ref,
     len_ref,
     hist_sem,
@@ -142,12 +143,36 @@
     total = users * cands
     pieces = seq // CHUNK
 
-    def rest(u):
-        part = pl.ds(0, seq - CHUNK)
-        return pltpu.make_async_copy(history_ref.at[u, part], hist_ref.at[u], hist_sem.at[u])
-
+    def fetch(j):
+        part = pl.ds(j * CHUNK, CHUNK)
+        return pltpu.make_async_copy(history_ref.at[:, part], hist_ref.at[:, part], hist_sem.at[j])
+
+    def begin(j, carry):
+        fetch(j).start()
+        return carry
+
+    lax.fori_loop(0, pieces - 1, begin, 0)
     for u in range(users):
         len_ref[u] = jnp.max(live_ref[users + u : users + u + 1, :]).astype(jnp.int32)
+
+    shift = pieces.bit_length() - 1
+    idle = users * pieces
+    waits = 2 * idle
+    items = jnp.int32(0)
+    met = []
+    for j in range(pieces - 1):
+        before = items
+        for u in range(users):
+            live = len_ref[u] > (j + 1) * CHUNK
+
+            @pl.when(live)
+            def _():
+                item_ref[items] = u * pieces + j + jnp.where(items == before, waits, 0)
+
+            items += live.astype(jnp.int32)
+        met.append(items > before)
+    for k in range(5):
+        item_ref[items + k] = idle
 
     group = answer_ref.shape[0] // 32
     got = answer_ref[...].astype(F32).reshape(group, 32, LANES)
@@ -171,18 +196,7 @@
             ).astype(BF16)
 
 
-    def begin(u, carry):
-        @pl.when(len_ref[u] > CHUNK)
-        def _():
-            rest(u).start()
-
-        return carry
-
-    lax.fori_loop(0, users, begin, 0)
-
     towers = (click_ref, convert_ref)
-    for k, hidden in enumerate(towers):
-        early_ref[k] = mm(joined_ref[:, width:], hidden[width:, :])
     lane = iota((1, CHUNK), 1)
 
     def exp_parts(scores_of, top):
@@ -194,51 +208,57 @@
             weight.append(w.astype(BF16))
         return jnp.concatenate(weight, axis=1), added
 
+    def last_score(u):
+        live = jnp.concatenate([live_ref[u : u + 1, :]] * (CHUNK // LANES), axis=1)
+        last_score_ref[u] = jnp.where(lane.astype(F32) < live, mm_nt(query_ref[u], last_ref[u]), NEG)
+
+    last_score(0)
     for u in range(users):
+        if u + 1 < users:
+            last_score(u + 1)
+        top = jnp.broadcast_to(jnp.max(last_score_ref[u], axis=1, keepdims=True), max_ref.shape[1:])
+        max_ref[u] = top
+        weight, sum_ref[u] = exp_parts(lambda part: last_score_ref[u, :, part], top)
         block = last_ref[u]
-        live = jnp.concatenate([live_ref[u : u + 1, :]] * (CHUNK // LANES), axis=1)
-        scores = jnp.where(lane.astype(F32) < live, mm_nt(query_ref[u], block), NEG)
-        top = jnp.broadcast_to(jnp.max(scores, axis=1, keepdims=True), (scores.shape[0], LANES))
-        max_ref[u] = top
-        weight, sum_ref[u] = exp_parts(lambda part: scores[:, part], top)
         acc_ref[u] = mm(weight, block)
 
-    def enter(k, user, source, offset, wait):
-        for field, value in enumerate((user, source, offset, wait)):
-            item_ref[field, k] = value
-
-    items = jnp.int32(0)
-    for u in range(users):
-        for j in range(1, pieces):
-
-            @pl.when(len_ref[u] > j * CHUNK)
-            def _():
-                enter(items + (j + 1), u, u, (j - 1) * CHUNK, int(j == 1))
-
-        items += lax.div(len_ref[u] - 1, CHUNK)
-    for k in (0, 1, *(items + (k + 2) for k in range(5))):
-        enter(k, users, 0, 0, 0)
+    for k, hidden in enumerate(towers):
+        early_ref[k] = mm(joined_ref[:, width:], hidden[width:, :])
 
     def entry(k):
-        return tuple(item_ref[field, k] for field in range(4))
+        code = item_ref[k]
+        user = lax.shift_right_logical(jnp.bitwise_and(code, waits - 1), shift)
+        return (
+            user,
+            jnp.minimum(user, users - 1),
+            jnp.bitwise_and(code, pieces - 1),
+            (code >= waits).astype(jnp.int32),
+        )
+
+    def arrive(item):
+        @pl.when(item[3] == 1)
+        def _():
+            fetch(item[2]).wait()
 
     def block(item):
-        return hist_ref[item[1], pl.ds(pl.multiple_of(item[2], CHUNK), CHUNK), :]
-
-    def step(now, ahead, beyond, score_to_ref, score_ref, weight_to_ref, scale_to_ref, weight_ref, scale_ref):
-        score_to_ref[...] = mm_nt(query_ref[beyond[1]], block(beyond))
-
-        u = ahead[0]
+        return hist_ref[item[1], pl.ds(pl.multiple_of(item[2] * CHUNK, CHUNK), CHUNK), :]
+
+    def score(item, score_ref):
+        score_ref[...] = mm_nt(query_ref[item[1]], block(item))
+
+    def weigh(item, score_ref, weight_ref, scale_ref):
+        u = item[0]
         old = max_ref[u]
         new = jnp.maximum(old, jnp.max(score_ref[...], axis=1, keepdims=True))
         scale = jnp.exp(old - new)
         max_ref[u] = new
-        scale_to_ref[...] = scale
-        weight_to_ref[...], added = exp_parts(lambda part: score_ref[:, part], new)
+        scale_ref[...] = scale
+        weight_ref[...], added = exp_parts(lambda part: score_ref[:, part], new)
         sum_ref[u] = sum_ref[u] * scale + added
 
-        u = now[0]
-        context = mm(weight_ref[...], block(now))
+    def gather(item, weight_ref, scale_ref):
+        u = item[0]
+        context = mm(weight_ref[...], block(item))
         scale = scale_ref[...]
         for k in range(width // LANES):
             part = slice(k * LANES, (k + 1) * LANES)
@@ -246,22 +266,40 @@
 
     def pair(p, carry):
         a, b, c, d = carry
-        for item in (c, d):
-
-            @pl.when(item[3] == 1)
-            def _():
-                rest(item[1]).wait()
-
-        step(a, b, c, score_a_ref, score_b_ref, weight_b_ref, scale_b_ref, weight_a_ref, scale_a_ref)
-        step(b, c, d, score_b_ref, score_a_ref, weight_a_ref, scale_a_ref, weight_b_ref, scale_b_ref)
+        arrive(c)
+        arrive(d)
+        score(c, score_a_ref)
+        weigh(b, score_b_ref, weight_b_ref, scale_b_ref)
+        gather(a, weight_a_ref, scale_a_ref)
+        score(d, score_b_ref)
+        weigh(c, score_a_ref, weight_a_ref, scale_a_ref)
+        gather(b, weight_b_ref, scale_b_ref)
         return c, d, entry(2 * p + 4), entry(2 * p + 5)
 
     @pl.when(items > 0)
     def _():
-        lax.fori_loop(0, lax.div(items + 3, 2), pair, tuple(entry(k) for k in range(4)))
-
-    row = iota((LANES, 1), 0)
-    nothing = jnp.zeros((LANES, width), F32)
+        begun = tuple(entry(k) for k in range(4))
+        arrive(begun[0])
+        arrive(begun[1])
+        score(begun[0], score_a_ref)
+        score(begun[1], score_b_ref)
+        weigh(begun[0], score_a_ref, weight_a_ref, scale_a_ref)
+        lax.fori_loop(0, lax.div(items + 1, 2) - 1, pair, begun)
+        last = entry(items - 1)
+        odd = jnp.bitwise_and(items, 1)
+
+        @pl.when(odd == 1)
+        def _():
+            gather(last, weight_a_ref, scale_a_ref)
+
+        @pl.when(odd == 0)
+        def _():
+            weigh(last, score_b_ref, weight_b_ref, scale_b_ref)
+            gather(entry(items - 2), weight_a_ref, scale_a_ref)
+            gather(last, weight_b_ref, scale_b_ref)
+
+    row = iota((16, 1), 0)
+    nothing = jnp.zeros((16, width), F32)
     click_out = jnp.where(row == 0, click_out_ref[...].astype(F32), nothing)
     convert_out = jnp.where(row == 1, convert_out_ref[...].astype(F32), nothing)
     out_weight = jnp.concatenate([click_out, convert_out], axis=1).astype(BF16)
@@ -295,12 +333,17 @@
             )
         )
     act = jnp.concatenate(act, axis=0)
-    logit = jnp.transpose(mm_nt(act, out_weight))
-    rate = jax.nn.sigmoid(logit[0:1])
-    both = rate * jax.nn.sigmoid(logit[1:2])
     for u in range(users):
-        rate_ref[u : u + 1, :] = rate[:, u * cands : (u + 1) * cands]
-        both_ref[u : u + 1, :] = both[:, u * cands : (u + 1) * cands]
+        logit = mm_nt(out_weight, act[u * cands : (u + 1) * cands])
+        chance = jax.nn.sigmoid(logit)
+        rate_ref[u : u + 1, :] = chance[0:1]
+        both_ref[u : u + 1, :] = chance[0:1] * chance[1:2]
+
+    for j in range(pieces - 1):
+
+        @pl.when(jnp.logical_not(met[j]))
+        def _():
+            fetch(j).wait()
 
 
 def earlier_rows(length):
@@ -456,9 +499,10 @@
             *[pltpu.VMEM((rows, CHUNK), BF16)] * 2,
             *[pltpu.VMEM((rows, LANES), F32)] * 2,
             pltpu.VMEM((2, total, click_hidden.shape[1]), F32),
-            pltpu.SMEM((4, users * (seq // CHUNK - 1) + 7), jnp.int32),
+            pltpu.VMEM((users, rows, CHUNK), F32),
+            pltpu.SMEM((users * (seq // CHUNK - 1) + 5,), jnp.int32),
             pltpu.SMEM((users,), jnp.int32),
-            pltpu.SemaphoreType.DMA((users,)),
+            pltpu.SemaphoreType.DMA((seq // CHUNK - 1,)),
         ],
         compiler_params=limit(24),
         name="attend",

time: 50 us -> 49.1 us (0.982)
  Pallas kernels: 13.1 us -> 12.5 us
    pallas_call x1, Pallas kernels: 4.73 us -> 4.17 us  [local(): pl.pallas_call(attend_kernel, out_shape=(jax.ShapeDtypeStruct((users, can...]
where the time goes in v3:
time: 49.1 us; the launch traced here: 48.8 us
  waiting for transfers between devices  18.9 us (38%)
  starting transfers between devices  16 us (33%)
  Pallas kernels  12.5 us (25%)
  between operations  0.72 us (1%)
  local copies, waits for them, and re-layouts  0.7 us (1%)
    all_to_all x1, waiting for transfers between devices, local(): answered = lax.all_to_all(answer, AXES, 0, 0, tiled=True)  11.4 us
    all_to_all x1, starting transfers between devices, local(): asked = lax.all_to_all(request, AXES, 0, 0, tiled=True)  11.2 us
    all_to_all x1, waiting for transfers between devices, local(): asked = lax.all_to_all(request, AXES, 0, 0, tiled=True)  7.56 us
    all_to_all x1, starting transfers between devices, local(): answered = lax.all_to_all(answer, AXES, 0, 0, tiled=True)  4.82 us
    pallas_call x1, Pallas kernels, local(): pl.pallas_call(attend_kernel, out_shape=(jax.ShapeDtypeStruct((users, can...  4.17 us
    pallas_call x1, Pallas kernels, local(): pl.pallas_call(answer_kernel, out_shape=jax.ShapeDtypeStruct((devices * 1...  3.44 us
    pallas_call x1, Pallas kernels, local(): pl.pallas_call(prepare_kernel, out_shape=(pltpu.VMEM((2 * users, LANES),...  2.09 us
    pallas_call x1, Pallas kernels, local(): pl.pallas_call(stage_kernel, out_shape=pltpu.VMEM((staged, row_width), BF...  1.75 us
  transfers between devices with their start and end apart: 2, of which 2 were waited for; matrix products, arithmetic and copies ran while one was open for 0% of the time, Pallas kernels for 8%

profile of v3, /device:TPU:0, one launch (start us, length us, event | category | flops | bytes accessed | tf_op | source)
XLA Modules:
  0.0 48.8 jit_solution(12045649318485993121)
XLA Ops:
  0.6 0.0 copy-start
  0.6 0.7 %copy-done = s32[4,64]{1,0:T(4,128)S(1)} copy-done((s32[4,64]{1,0:T(4,128)S(1)}, s32[4,64]{1,0:T(4,128)}, u32[]{:S(2)}) %copy-start) | copy-done | bytes 1048
  1.3 1.1 %request.1 = (f32[128,128]{1,0:T(8,128)}, f32[8,256]{1,0:T(8,128)S(1)}) custom-call(s32[4,64]{1,0:T(4,128)S(1)} %copy-done), custom_call_target="tpu_custom_call" | custom-call | tf_op jit(solution)/shard_map/request/pallas_call | solution.py:442
  2.4 11.2 %all-to-all-start = ((f32[128,1,128]{2,1,0:T(1,128)}), f32[128,1,128]{2,1,0:T(1,128)S(1)}, u32[]{:S(2)}, u32[]{:S(2)}) async-start(f32[128,1,128]{2,1,0:T(1,128)} %bitcast.1), calls=%async_computation | async-start | bytes 131072 | tf_op jit(solution)/shard_map/all_to_all | solution.py:450
  13.5 1.8 %stage.1.staged_ref = bf16[2560,512]{1,0:T(8,128)(2,1)S(1)} custom-call(bf16[4096,512]{1,0:T(8,128)(2,1)} %table_ref.1), custom_call_target="tpu_custom_call" | custom-call | flops 1073741824 | bytes 4194304 | tf_op jit(solution)/shard_map/stage/pallas_call | solution.py:432
  15.3 7.6 %all-to-all-done = f32[128,1,128]{2,1,0:T(1,128)S(1)} async-done(((f32[128,1,128]{2,1,0:T(1,128)}), f32[128,1,128]{2,1,0:T(1,128)S(1)}, u32[]{:S(2)}, u32[]{:S(2)}) %all-to-all-start) | async-done | bytes 65568 | tf_op jit(solution)/shard_map/all_to_all | solution.py:450
  22.9 0.0 copy-start.2
  22.9 0.0 copy-start.3
  22.9 0.0 copy-start.1
  22.9 3.4 %answer.1 = bf16[2048,128]{1,0:T(8,128)(2,1)} custom-call(f32[128,128]{1,0:T(8,128)S(1)} %bitcast.7, bf16[2560,512]{1,0:T(8,128)(2,1)S(1)} %stage.1.staged_ref, bf16[4096,512]{1,0:T(8,128)(2,1)} %table_ref.1), custom_call_target="tpu_custom_call" | custom-call | tf_op jit(solution)/shard_map/answer/pallas_call | solution.py:451
  26.3 4.8 %all-to-all-start.1 = ((bf16[128,16,128]{2,1,0:T(8,128)(2,1)}), bf16[128,16,128]{2,1,0:T(8,128)(2,1)S(1)}, u32[]{:S(2)}, u32[]{:S(2)}) async-start(bf16[128,16,128]{2,1,0:T(8,128)(2,1)} %bitcast.3), calls=%async_computation.1 | async-start | bytes 1048576 | tf_op jit(solution)/shard_map/all_to_all | solution.py:466
  31.1 0.0 copy-done.2
  31.2 0.0 copy-done.3
  31.2 0.0 copy-done.1
  31.2 2.1 %prepare.1 = (f32[8,128]{1,0:T(8,128)S(1)}, bf16[256,512]{1,0:T(8,128)(2,1)S(1)}, bf16[4,512,256]{2,1,0:T(8,128)(2,1)S(1)}, bf16[256,256]{1,0:T(8,128)(2,1)S(1)}...) custom-call(s32[4]{0:T(128)S(1)} %copy-done.1, f32[8,256]{1,0:T(8,128)S(1)} %get-tuple-element.10.slot_ref, ...), custom_call_target="tpu_custom_call" | custom-call | flops 1073741824 | bytes 4194304 | tf_op jit(solution)/shard_map/prepare/pallas_call | solution.py:467
  33.3 11.4 %all-to-all-done.1 = bf16[128,16,128]{2,1,0:T(8,128)(2,1)S(1)} async-done(((bf16[128,16,128]{2,1,0:T(8,128)(2,1)}), bf16[128,16,128]{2,1,0:T(8,128)(2,1)S(1)}, u32[]{:S(2)}, u32[]{:S(2)}) %all-to-all-start.1) | async-done | bytes 524320 | tf_op jit(solution)/shard_map/all_to_all | solution.py:466
  44.6 4.2 %attend.1 = (f32[4,64]{1,0:T(4,128)}, f32[4,64]{1,0:T(4,128)}) custom-call(f32[8,128]{1,0:T(8,128)S(1)} %get-tuple-element.11.live_ref, bf16[256,512]{1,0:T(8,128)(2,1)S(1)} %get-tuple-element.12.pick_ref, bf16[2048,128]{1,0:T(8,128)(2,1)S(1)} %bitcast.6, bf16[4,512,256]{2,1,0:T(8,128)(2,1)S(1)} %get-tuple-element.14.last_ref, ...), custom_call_target="tpu_custom_call" | custom-call | tf_op jit(solution)/shard_map/attend/pallas_call | solution.py:483
  (2 shorter events, 0.0 us)
Async XLA Ops:
  0.6 0.7 %copy-start = (s32[4,64]{1,0:T(4,128)S(1)}, s32[4,64]{1,0:T(4,128)}, u32[]{:S(2)}) copy-start(s32[4,64]{1,0:T(4,128)} %cand_ref.1) | copy-start | bytes 3076
  2.4 20.5 %all-to-all-start = ((f32[128,1,128]{2,1,0:T(1,128)}), f32[128,1,128]{2,1,0:T(1,128)S(1)}, u32[]{:S(2)}, u32[]{:S(2)}) async-start(f32[128,1,128]{2,1,0:T(1,128)} %bitcast.1), calls=%async_computation | async-start | bytes 131072 | tf_op jit(solution)/shard_map/all_to_all | solution.py:450
  22.9 8.3 %copy-start.2 = (bf16[256]{0:T(256)(128)(2,1)S(1)}, bf16[256]{0:T(256)(128)(2,1)}, u32[]{:S(2)}) copy-start(bf16[256]{0:T(256)(128)(2,1)} %param.16) | copy-start | bytes 1540
  22.9 8.3 %copy-start.3 = (bf16[256]{0:T(256)(128)(2,1)S(1)}, bf16[256]{0:T(256)(128)(2,1)}, u32[]{:S(2)}) copy-start(bf16[256]{0:T(256)(128)(2,1)} %param.17) | copy-start | bytes 1540
  22.9 8.3 %copy-start.1 = (s32[4]{0:T(128)S(1)}, s32[4]{0:T(128)}, u32[]{:S(2)}) copy-start(s32[4]{0:T(128)} %len_ref.1) | copy-start | bytes 52
  26.3 18.3 %all-to-all-start.1 = ((bf16[128,16,128]{2,1,0:T(8,128)(2,1)}), bf16[128,16,128]{2,1,0:T(8,128)(2,1)S(1)}, u32[]{:S(2)}, u32[]{:S(2)}) async-start(bf16[128,16,128]{2,1,0:T(8,128)(2,1)} %bitcast.3), calls=%async_computation.1 | async-start | bytes 1048576 | tf_op jit(solution)/shard_map/all_to_all | solution.py:466

commit v4 on v3

--- a/solution.py
+++ b/solution.py
@@ -58,18 +58,16 @@
     req_ref[...] = mm_nt(jnp.concatenate(picks, axis=1), jnp.concatenate(values, axis=1))
 
 
-def answer_kernel(req_ref, staged_ref, table_ref, out_ref, hot_ref, high_ref, acc_ref, rest_ref, sem_ref):
+def answer_kernel(req_ref, staged_ref, spread_ref, which_ref, table_ref, out_ref, hot_ref, high_ref, acc_ref, rest_ref, sem_ref):
     sources = req_ref.shape[0]
     rows = sources * SLOTS
     staged, width = staged_ref.shape
     rest = pltpu.make_async_copy(table_ref.at[pl.ds(staged, rest_ref.shape[0])], rest_ref, sem_ref)
     rest.start()
-    spread = ones_where(lax.shift_right_logical(iota((rows, sources), 0), 2) == iota((rows, sources), 1))
-    asked = mm(spread, req_ref[...].astype(BF16))
+    asked = mm(spread_ref[...], req_ref[...].astype(BF16))
     own = lax.shift_right_logical(iota((rows, LANES), 1), 1) == jnp.bitwise_and(iota((rows, LANES), 0), 3)
     asked = jnp.where(own, asked, 0.0).astype(BF16)
-    which = jnp.bitwise_and(iota((LANES, 512), 0), 1) == lax.shift_right_logical(iota((LANES, 512), 1), 8)
-    both = mm(asked, ones_where(which))
+    both = mm(asked, which_ref[...])
     high_ref[...] = both[:, :256].astype(BF16)
     hot_ref[...] = ones_where(both[:, 256:] == iota((rows, 256), 1).astype(F32))
 
@@ -350,9 +348,14 @@
     return lax.div(length - 1, CHUNK) * CHUNK
 
 
-def stage_kernel(from_ref, to_ref, sem_ref):
+def stage_kernel(from_ref, to_ref, spread_ref, which_ref, sem_ref):
     copy = pltpu.make_async_copy(from_ref.at[pl.ds(0, to_ref.shape[0])], to_ref, sem_ref)
     copy.start()
+    shape = spread_ref.shape
+    spread_ref[...] = ones_where(lax.shift_right_logical(iota(shape, 0), 2) == iota(shape, 1))
+    shape = which_ref.shape
+    which = jnp.bitwise_and(iota(shape, 0), 1) == lax.shift_right_logical(iota(shape, 1), 8)
+    which_ref[...] = ones_where(which)
     copy.wait()
 
 
@@ -431,9 +434,13 @@
 
     table_start = pl.pallas_call(
         stage_kernel,
-        out_shape=pltpu.VMEM((staged, row_width), BF16),
+        out_shape=(
+            pltpu.VMEM((staged, row_width), BF16),
+            pltpu.VMEM((devices * SLOTS, devices), BF16),
+            pltpu.VMEM((LANES, 512), BF16),
+        ),
         in_specs=[hbm()],
-        out_specs=vmem(),
+        out_specs=(vmem(),) * 3,
         scratch_shapes=[pltpu.SemaphoreType.DMA(())],
         cost_estimate=window_cost(2 * table.size),
         compiler_params=limit(2),
@@ -451,7 +458,7 @@
     answer = pl.pallas_call(
         answer_kernel,
         out_shape=jax.ShapeDtypeStruct((devices * 16, LANES), BF16),
-        in_specs=[vmem(), vmem(), hbm()],
+        in_specs=[vmem()] * 4 + [hbm()],
         out_specs=vmem(),
         scratch_shapes=[
             pltpu.VMEM((devices * SLOTS, 256), BF16),
@@ -462,7 +469,7 @@
         ],
         compiler_params=limit(24),
         name="answer",
-    )(asked, in_vmem(table_start), table)
+    )(asked, *(in_vmem(x) for x in table_start), table)
     answered = lax.all_to_all(answer, AXES, 0, 0, tiled=True)
     prepared = pl.pallas_call(
         prepare_kernel,

time: 49.1 us -> 49 us (level)
  no operation moved by 1% of the time
where the time goes in v4:
time: 49 us; the launch traced here: 48.7 us
  waiting for transfers between devices  18.9 us (39%)
  starting transfers between devices  16 us (33%)
  Pallas kernels  12.4 us (25%)
  between operations  0.72 us (1%)
  local copies, waits for them, and re-layouts  0.7 us (1%)
    all_to_all x1, waiting for transfers between devices, local(): answered = lax.all_to_all(answer, AXES, 0, 0, tiled=True)  11.4 us
    all_to_all x1, starting transfers between devices, local(): asked = lax.all_to_all(request, AXES, 0, 0, tiled=True)  11.2 us
    all_to_all x1, waiting for transfers between devices, local(): asked = lax.all_to_all(request, AXES, 0, 0, tiled=True)  7.56 us
    all_to_all x1, starting transfers between devices, local(): answered = lax.all_to_all(answer, AXES, 0, 0, tiled=True)  4.8 us
    pallas_call x1, Pallas kernels, local(): pl.pallas_call(attend_kernel, out_shape=(jax.ShapeDtypeStruct((users, can...  4.1 us
    pallas_call x1, Pallas kernels, local(): pl.pallas_call(answer_kernel, out_shape=jax.ShapeDtypeStruct((devices * 1...  3.43 us
    pallas_call x1, Pallas kernels, local(): pl.pallas_call(prepare_kernel, out_shape=(pltpu.VMEM((2 * users, LANES),...  2.09 us
    pallas_call x1, Pallas kernels, local(): pl.pallas_call(stage_kernel, out_shape=(pltpu.VMEM((staged, row_width), B...  1.75 us
  transfers between devices with their start and end apart: 2, of which 2 were waited for; matrix products, arithmetic and copies ran while one was open for 0% of the time, Pallas kernels for 8%

profile of v4, /device:TPU:0, one launch (start us, length us, event | category | flops | bytes accessed | tf_op | source)
XLA Modules:
  0.0 48.7 jit_solution(6538559110768509956)
XLA Ops:
  0.6 0.0 copy-start
  0.6 0.7 %copy-done = s32[4,64]{1,0:T(4,128)S(1)} copy-done((s32[4,64]{1,0:T(4,128)S(1)}, s32[4,64]{1,0:T(4,128)}, u32[]{:S(2)}) %copy-start) | copy-done | bytes 1048
  1.3 1.1 %request.1 = (f32[128,128]{1,0:T(8,128)}, f32[8,256]{1,0:T(8,128)S(1)}) custom-call(s32[4,64]{1,0:T(4,128)S(1)} %copy-done), custom_call_target="tpu_custom_call" | custom-call | tf_op jit(solution)/shard_map/request/pallas_call | solution.py:449
  2.4 11.2 %all-to-all-start = ((f32[128,1,128]{2,1,0:T(1,128)}), f32[128,1,128]{2,1,0:T(1,128)S(1)}, u32[]{:S(2)}, u32[]{:S(2)}) async-start(f32[128,1,128]{2,1,0:T(1,128)} %bitcast.1), calls=%async_computation | async-start | bytes 131072 | tf_op jit(solution)/shard_map/all_to_all | solution.py:457
  13.5 1.8 %stage.1 = (bf16[2560,512]{1,0:T(8,128)(2,1)S(1)}, bf16[512,128]{1,0:T(8,128)(2,1)S(1)}, bf16[128,512]{1,0:T(8,128)(2,1)S(1)}) custom-call(bf16[4096,512]{1,0:T(8,128)(2,1)} %table_ref.1), custom_call_target="tpu_custom_call" | custom-call | flops 1073741824 | bytes 4194304 | tf_op jit(solution)/shard_map/stage/pallas_call | solution.py:435
  15.3 7.6 %all-to-all-done = f32[128,1,128]{2,1,0:T(1,128)S(1)} async-done(((f32[128,1,128]{2,1,0:T(1,128)}), f32[128,1,128]{2,1,0:T(1,128)S(1)}, u32[]{:S(2)}, u32[]{:S(2)}) %all-to-all-start) | async-done | bytes 65568 | tf_op jit(solution)/shard_map/all_to_all | solution.py:457
  22.9 0.0 copy-start.2
  22.9 0.0 copy-start.3
  22.9 0.0 copy-start.1
  22.9 3.4 %answer.1 = bf16[2048,128]{1,0:T(8,128)(2,1)} custom-call(f32[128,128]{1,0:T(8,128)S(1)} %bitcast.7, bf16[2560,512]{1,0:T(8,128)(2,1)S(1)} %get-tuple-element.17.staged_ref, bf16[512,128]{1,0:T(8,128)(2,1)S(1)} %get-tuple-element.18.spread_ref, bf16[128,512]{1,0:T(8,128)(2,1)S(1)} %get-tuple-element.19.which_ref, bf16[4096,512]{1,0:T(8,128)(2,1)} %table_ref.1), custom_call_target="tpu_custom_call" | custom-call | tf_op jit(solution)/shard_map/answer/pallas_call | solution.py:458
  26.3 4.8 %all-to-all-start.1 = ((bf16[128,16,128]{2,1,0:T(8,128)(2,1)}), bf16[128,16,128]{2,1,0:T(8,128)(2,1)S(1)}, u32[]{:S(2)}, u32[]{:S(2)}) async-start(bf16[128,16,128]{2,1,0:T(8,128)(2,1)} %bitcast.3), calls=%async_computation.1 | async-start | bytes 1048576 | tf_op jit(solution)/shard_map/all_to_all | solution.py:473
  31.1 0.0 copy-done.2
  31.1 0.0 copy-done.3
  31.2 0.0 copy-done.1
  31.2 2.1 %prepare.1 = (f32[8,128]{1,0:T(8,128)S(1)}, bf16[256,512]{1,0:T(8,128)(2,1)S(1)}, bf16[4,512,256]{2,1,0:T(8,128)(2,1)S(1)}, bf16[256,256]{1,0:T(8,128)(2,1)S(1)}...) custom-call(s32[4]{0:T(128)S(1)} %copy-done.1, f32[8,256]{1,0:T(8,128)S(1)} %get-tuple-element.13.slot_ref, ...), custom_call_target="tpu_custom_call" | custom-call | flops 1073741824 | bytes 4194304 | tf_op jit(solution)/shard_map/prepare/pallas_call | solution.py:474
  33.3 11.4 %all-to-all-done.1 = bf16[128,16,128]{2,1,0:T(8,128)(2,1)S(1)} async-done(((bf16[128,16,128]{2,1,0:T(8,128)(2,1)}), bf16[128,16,128]{2,1,0:T(8,128)(2,1)S(1)}, u32[]{:S(2)}, u32[]{:S(2)}) %all-to-all-start.1) | async-done | bytes 524320 | tf_op jit(solution)/shard_map/all_to_all | solution.py:473
  44.6 4.1 %attend.1 = (f32[4,64]{1,0:T(4,128)}, f32[4,64]{1,0:T(4,128)}) custom-call(f32[8,128]{1,0:T(8,128)S(1)} %get-tuple-element.14.live_ref, bf16[256,512]{1,0:T(8,128)(2,1)S(1)} %get-tuple-element.15.pick_ref, bf16[2048,128]{1,0:T(8,128)(2,1)S(1)} %bitcast.6, bf16[4,512,256]{2,1,0:T(8,128)(2,1)S(1)} %get-tuple-element.20.last_ref, ...), custom_call_target="tpu_custom_call" | custom-call | tf_op jit(solution)/shard_map/attend/pallas_call | solution.py:490
  (2 shorter events, 0.0 us)
Async XLA Ops:
  0.6 0.7 %copy-start = (s32[4,64]{1,0:T(4,128)S(1)}, s32[4,64]{1,0:T(4,128)}, u32[]{:S(2)}) copy-start(s32[4,64]{1,0:T(4,128)} %cand_ref.1) | copy-start | bytes 3076
  2.4 20.5 %all-to-all-start = ((f32[128,1,128]{2,1,0:T(1,128)}), f32[128,1,128]{2,1,0:T(1,128)S(1)}, u32[]{:S(2)}, u32[]{:S(2)}) async-start(f32[128,1,128]{2,1,0:T(1,128)} %bitcast.1), calls=%async_computation | async-start | bytes 131072 | tf_op jit(solution)/shard_map/all_to_all | solution.py:457
  22.9 8.3 %copy-start.2 = (bf16[256]{0:T(256)(128)(2,1)S(1)}, bf16[256]{0:T(256)(128)(2,1)}, u32[]{:S(2)}) copy-start(bf16[256]{0:T(256)(128)(2,1)} %param.16) | copy-start | bytes 1540
  22.9 8.3 %copy-start.3 = (bf16[256]{0:T(256)(128)(2,1)S(1)}, bf16[256]{0:T(256)(128)(2,1)}, u32[]{:S(2)}) copy-start(bf16[256]{0:T(256)(128)(2,1)} %param.17) | copy-start | bytes 1540
  22.9 8.3 %copy-start.1 = (s32[4]{0:T(128)S(1)}, s32[4]{0:T(128)}, u32[]{:S(2)}) copy-start(s32[4]{0:T(128)} %len_ref.1) | copy-start | bytes 52
  26.3 18.3 %all-to-all-start.1 = ((bf16[128,16,128]{2,1,0:T(8,128)(2,1)}), bf16[128,16,128]{2,1,0:T(8,128)(2,1)S(1)}, u32[]{:S(2)}, u32[]{:S(2)}) async-start(bf16[128,16,128]{2,1,0:T(8,128)(2,1)} %bitcast.3), calls=%async_computation.1 | async-start | bytes 1048576 | tf_op jit(solution)/shard_map/all_to_all | solution.py:473

commit v5 on v3

--- a/solution.py
+++ b/solution.py
@@ -35,17 +35,20 @@
     return lax.dot_general(a, b, (((1,), (1,)), ((), ())), preferred_element_type=F32)
 
 
-def request_kernel(cand_ref, req_ref, slot_ref, *, owners, row_bits):
+def request_kernel(cand_hbm_ref, req_ref, slot_ref, cand_ref, before_ref, sem_ref, *, owners, row_bits):
     users, cands = cand_ref.shape
     total = users * cands
+    arrival = pltpu.make_async_copy(cand_hbm_ref, cand_ref, sem_ref)
+    arrival.start()
+    before_ref[...] = ones_where(iota((total, total), 0) < iota((total, total), 1))
+    arrival.wait()
     ids = jnp.concatenate([cand_ref[u : u + 1, :] for u in range(users)], axis=1)
     owner = lax.shift_right_logical(ids, row_bits)
     row = jnp.bitwise_and(ids, (1 << row_bits) - 1)
     high = lax.shift_right_logical(row, 8).astype(F32)
     low = jnp.bitwise_and(row, 255).astype(F32)
     match = iota((owners, total), 0) == owner
-    before = ones_where(iota((total, total), 0) < iota((total, total), 1))
-    rank = mm(ones_where(match), before)
+    rank = mm(ones_where(match), before_ref[...])
     place = jnp.sum(jnp.where(match, rank, 0.0), axis=0, keepdims=True) + (owner * SLOTS).astype(F32)
     slot_ref[...] = jnp.broadcast_to(place, slot_ref.shape)
     lane = iota((LANES, total), 0)
@@ -442,11 +445,16 @@
     request, place = pl.pallas_call(
         functools.partial(request_kernel, owners=devices, row_bits=table_rows.bit_length() - 1),
         out_shape=(pltpu.VMEM((devices, LANES), F32), pltpu.VMEM((8, total), F32)),
-        in_specs=[vmem()],
+        in_specs=[hbm()],
         out_specs=(vmem(), vmem()),
+        scratch_shapes=[
+            pltpu.VMEM(candidates.shape, jnp.int32),
+            pltpu.VMEM((total, total), BF16),
+            pltpu.SemaphoreType.DMA(()),
+        ],
         compiler_params=limit(8),
         name="request",
-    )(candidates)
+    )(in_hbm(candidates))
     asked = lax.all_to_all(request, AXES, 0, 0, tiled=True)
     answer = pl.pallas_call(
         answer_kernel,

time: 49.1 us -> 49.4 us (level)
  Pallas kernels: 12.5 us -> 13.5 us
  local copies, waits for them, and re-layouts: 0.7 us -> 0.02 us
    pallas_call x1, Pallas kernels: 1.05 us -> 1.75 us  [local(): pl.pallas_call(functools.partial(request_kernel, owners=devices, row_bits...]
    unnamed x8 -> x6, local copies, waits for them, and re-layouts: 0.69 us -> 0.01 us
where the time goes in v5:
time: 49.4 us; the launch traced here: 49.1 us
  waiting for transfers between devices  18.9 us (38%)
  starting transfers between devices  16 us (32%)
  Pallas kernels  13.5 us (27%)
  between operations  0.72 us (1%)
    all_to_all x1, waiting for transfers between devices, local(): answered = lax.all_to_all(answer, AXES, 0, 0, tiled=True)  11.4 us
    all_to_all x1, starting transfers between devices, local(): asked = lax.all_to_all(request, AXES, 0, 0, tiled=True)  11.2 us
    all_to_all x1, waiting for transfers between devices, local(): asked = lax.all_to_all(request, AXES, 0, 0, tiled=True)  7.54 us
    all_to_all x1, starting transfers between devices, local(): answered = lax.all_to_all(answer, AXES, 0, 0, tiled=True)  4.82 us
    pallas_call x1, Pallas kernels, local(): pl.pallas_call(attend_kernel, out_shape=(jax.ShapeDtypeStruct((users, can...  4.42 us
    pallas_call x1, Pallas kernels, local(): pl.pallas_call(answer_kernel, out_shape=jax.ShapeDtypeStruct((devices * 1...  3.44 us
    pallas_call x1, Pallas kernels, local(): pl.pallas_call(prepare_kernel, out_shape=(pltpu.VMEM((2 * users, LANES),...  2.09 us
    pallas_call x1, Pallas kernels, local(): pl.pallas_call(functools.partial(request_kernel, owners=devices, row_bits...  1.75 us
  transfers between devices with their start and end apart: 2, of which 2 were waited for; matrix products, arithmetic and copies ran while one was open for 0% of the time, Pallas kernels for 8%

profile of v5, /device:TPU:0, one launch (start us, length us, event | category | flops | bytes accessed | tf_op | source)
XLA Modules:
  0.0 49.1 jit_solution(769309462219273536)
XLA Ops:
  0.6 1.8 %request.1 = (f32[128,128]{1,0:T(8,128)}, f32[8,256]{1,0:T(8,128)S(1)}) custom-call(s32[4,64]{1,0:T(4,128)} %cand_hbm_ref.1), custom_call_target="tpu_custom_call" | custom-call | tf_op jit(solution)/shard_map/request/pallas_call | solution.py:445
  2.4 11.2 %all-to-all-start = ((f32[128,1,128]{2,1,0:T(1,128)}), f32[128,1,128]{2,1,0:T(1,128)S(1)}, u32[]{:S(2)}, u32[]{:S(2)}) async-start(f32[128,1,128]{2,1,0:T(1,128)} %bitcast.1), calls=%async_computation | async-start | bytes 131072 | tf_op jit(solution)/shard_map/all_to_all | solution.py:458
  13.6 1.8 %stage.1.staged_ref = bf16[2560,512]{1,0:T(8,128)(2,1)S(1)} custom-call(bf16[4096,512]{1,0:T(8,128)(2,1)} %table_ref.1), custom_call_target="tpu_custom_call" | custom-call | flops 1073741824 | bytes 4194304 | tf_op jit(solution)/shard_map/stage/pallas_call | solution.py:435
  15.3 7.5 %all-to-all-done = f32[128,1,128]{2,1,0:T(1,128)S(1)} async-done(((f32[128,1,128]{2,1,0:T(1,128)}), f32[128,1,128]{2,1,0:T(1,128)S(1)}, u32[]{:S(2)}, u32[]{:S(2)}) %all-to-all-start) | async-done | bytes 65568 | tf_op jit(solution)/shard_map/all_to_all | solution.py:458
  22.9 0.0 copy-start.1
  22.9 0.0 copy-start.2
  22.9 0.0 copy-start
  22.9 3.4 %answer.1 = bf16[2048,128]{1,0:T(8,128)(2,1)} custom-call(f32[128,128]{1,0:T(8,128)S(1)} %bitcast.7, bf16[2560,512]{1,0:T(8,128)(2,1)S(1)} %stage.1.staged_ref, bf16[4096,512]{1,0:T(8,128)(2,1)} %table_ref.1), custom_call_target="tpu_custom_call" | custom-call | tf_op jit(solution)/shard_map/answer/pallas_call | solution.py:459
  26.3 4.8 %all-to-all-start.1 = ((bf16[128,16,128]{2,1,0:T(8,128)(2,1)}), bf16[128,16,128]{2,1,0:T(8,128)(2,1)S(1)}, u32[]{:S(2)}, u32[]{:S(2)}) async-start(bf16[128,16,128]{2,1,0:T(8,128)(2,1)} %bitcast.3), calls=%async_computation.1 | async-start | bytes 1048576 | tf_op jit(solution)/shard_map/all_to_all | solution.py:474
  31.2 0.0 copy-done.1
  31.2 0.0 copy-done.2
  31.2 0.0 copy-done
  31.2 2.1 %prepare.1 = (f32[8,128]{1,0:T(8,128)S(1)}, bf16[256,512]{1,0:T(8,128)(2,1)S(1)}, bf16[4,512,256]{2,1,0:T(8,128)(2,1)S(1)}, bf16[256,256]{1,0:T(8,128)(2,1)S(1)}...) custom-call(s32[4]{0:T(128)S(1)} %copy-done, f32[8,256]{1,0:T(8,128)S(1)} %get-tuple-element.10.slot_ref, ...), custom_call_target="tpu_custom_call" | custom-call | flops 1073741824 | bytes 4194304 | tf_op jit(solution)/shard_map/prepare/pallas_call | solution.py:475
  33.3 11.4 %all-to-all-done.1 = bf16[128,16,128]{2,1,0:T(8,128)(2,1)S(1)} async-done(((bf16[128,16,128]{2,1,0:T(8,128)(2,1)}), bf16[128,16,128]{2,1,0:T(8,128)(2,1)S(1)}, u32[]{:S(2)}, u32[]{:S(2)}) %all-to-all-start.1) | async-done | bytes 524320 | tf_op jit(solution)/shard_map/all_to_all | solution.py:474
  44.7 4.4 %attend.1 = (f32[4,64]{1,0:T(4,128)}, f32[4,64]{1,0:T(4,128)}) custom-call(f32[8,128]{1,0:T(8,128)S(1)} %get-tuple-element.11.live_ref, bf16[256,512]{1,0:T(8,128)(2,1)S(1)} %get-tuple-element.12.pick_ref, bf16[2048,128]{1,0:T(8,128)(2,1)S(1)} %bitcast.6, bf16[4,512,256]{2,1,0:T(8,128)(2,1)S(1)} %get-tuple-element.14.last_ref, ...), custom_call_target="tpu_custom_call" | custom-call | tf_op jit(solution)/shard_map/attend/pallas_call | solution.py:491
  (2 shorter events, 0.0 us)
Async XLA Ops:
  2.4 20.5 %all-to-all-start = ((f32[128,1,128]{2,1,0:T(1,128)}), f32[128,1,128]{2,1,0:T(1,128)S(1)}, u32[]{:S(2)}, u32[]{:S(2)}) async-start(f32[128,1,128]{2,1,0:T(1,128)} %bitcast.1), calls=%async_computation | async-start | bytes 131072 | tf_op jit(solution)/shard_map/all_to_all | solution.py:458
  22.9 8.3 %copy-start.1 = (bf16[256]{0:T(256)(128)(2,1)S(1)}, bf16[256]{0:T(256)(128)(2,1)}, u32[]{:S(2)}) copy-start(bf16[256]{0:T(256)(128)(2,1)} %param.16) | copy-start | bytes 1540
  22.9 8.3 %copy-start.2 = (bf16[256]{0:T(256)(128)(2,1)S(1)}, bf16[256]{0:T(256)(128)(2,1)}, u32[]{:S(2)}) copy-start(bf16[256]{0:T(256)(128)(2,1)} %param.17) | copy-start | bytes 1540
  22.9 8.3 %copy-start = (s32[4]{0:T(128)S(1)}, s32[4]{0:T(128)}, u32[]{:S(2)}) copy-start(s32[4]{0:T(128)} %len_ref.1) | copy-start | bytes 52
  26.3 18.3 %all-to-all-start.1 = ((bf16[128,16,128]{2,1,0:T(8,128)(2,1)}), bf16[128,16,128]{2,1,0:T(8,128)(2,1)S(1)}, u32[]{:S(2)}, u32[]{:S(2)}) async-start(bf16[128,16,128]{2,1,0:T(8,128)(2,1)} %bitcast.3), calls=%async_computation.1 | async-start | bytes 1048576 | tf_op jit(solution)/shard_map/all_to_all | solution.py:474
